TPU v7x, 128 devices: a whole 4x4x4 slice. The times are simulated.
128 devices in a mesh: px: 16 (over x, z_hi, core), py: 8 (over z_lo, y).
Axes of the slice: x: 4, y: 4, z: 4 (z_hi: 2, z_lo: 2; z = z_hi * 2 + z_lo), core: 2. Of those that a mesh axis runs over, the one named last changes fastest.
Arguments:
- state: float32 [4, 128, 16, 4096], P(None, ('px', 'py')), may hold values from -6 to 6
- past_slow: float32 [4, 128, 16, 4096], P(None, ('px', 'py')), may hold values from -6 to 6
- mean_wind: float32 [128], P(('px', 'py')), may hold values from -2 to 2
- damping: float32 [128], P(('px', 'py')), may hold values from 0.05 to 1
- vertical_inverse: float32 [256, 256], replicated, as said below
- section: int32 [8], replicated, may hold values from 0 to 3
Outputs:
- advanced: float32 [4, 128, 16, 4096], P(None, ('px', 'py'))
Inputs may be any that keep to these rules, and one draw needn't show every extreme that they name: `section`: row of the four-row coupling coefficient table for each substep. `vertical_inverse`: the inverse of a nonsingular vertical acoustic operator for 128 levels of vertical velocity followed by 128 levels of pressure.
All inputs are finite; a program needn't handle non-finite values.
Results may differ from a plain program's by a relative error of at most 0.00015.
Values sent between devices are 32-bit elements; how exact they have to be, the bound alone decides.
No kernel may reach another device: no remote copies, remote signals or barrier semaphores. Data moves between devices by JAX's collectives and lax.ppermute only.
A program may use at most 128 MiB of HBM per device.

v0:
```python
import math

import jax
import jax.numpy as jnp
import numpy as np
from jax import lax
from jax.experimental import pallas as pl
from jax.experimental.pallas import tpu as pltpu
from jax.sharding import PartitionSpec as P

SUBSTEPS = 8
NX, NY, NZ = 4096, 16, 128
N1, N2 = 32, 128
KAP = NY // 2
HALF = 0.275
FAST = 1.0 / SUBSTEPS
NOW = (-1.0, 2.0, 0.5, 1.5)
PAST = (1.0, -0.5, 0.25, -1.0)
ROWS_IN = 25
ROWS_OUT = 12

f32 = jnp.float32
bf16 = jnp.bfloat16


def halves(table):
    high = jnp.asarray(table, f32).astype(bf16)
    low = jnp.asarray(np.asarray(table, np.float64) - np.asarray(high, np.float64), bf16)
    return np.stack([np.asarray(high), np.asarray(low)])


def tables():
    n1 = np.arange(N1)
    y = np.arange(NY)
    kap = np.arange(KAP)
    qa = np.cos(2 * np.pi * kap[:, None] * y[None, :] / NY) * math.sqrt(2.0 / NY)
    qb = np.sin(2 * np.pi * kap[:, None] * y[None, :] / NY) * math.sqrt(2.0 / NY)
    qa[0] = 1.0 / math.sqrt(NY)
    qb[0] = (-1.0) ** y / math.sqrt(NY)
    q = qa + 1j * qb
    dft1 = np.exp(-2j * np.pi * (n1[:, None] * n1[None, :] % N1) / N1)
    stage = np.einsum("kn,cy->kcny", dft1, q).reshape(N1, KAP, N1, 2, 8)
    stage = stage.transpose(0, 1, 3, 2, 4).reshape(N1 * KAP, 2 * N1 * 8)
    first = np.concatenate([stage.real, stage.imag], 0)
    last = first.T / NX
    n2 = np.arange(N2)
    angle = 2 * np.pi * (n2[:, None] * n2[None, :] % N2) / N2
    cos, sin = np.cos(angle), np.sin(angle)
    second = np.block([[cos, sin], [-sin, cos]])
    turn = 2 * np.pi * (n1[:, None] * n2[None, :]) / NX
    twist = np.stack([np.cos(turn), np.sin(turn)]).astype(np.float32)
    wide = np.repeat(turn.T, KAP, axis=1)
    untwist = np.stack([np.cos(wide), np.sin(wide)]).astype(np.float32)
    return halves(first), halves(last), halves(second), halves(second.T), twist, untwist


FIRST, LAST, SECOND, SECOND_BACK, TWIST, UNTWIST = tables()


def split(value):
    high = value.astype(bf16)
    return high, (value - high.astype(f32)).astype(bf16)


def product(left, right, dims=((1,), (0,))):
    def dot(a, b):
        return lax.dot_general(a, b, (dims, ((), ())), preferred_element_type=f32)

    return dot(left[0], right[0]) + (dot(left[1], right[0]) + dot(left[0], right[1]))


ACROSS = ((1,), (1,))


def tiles(plane):
    return jnp.concatenate(
        [plane[8 * b : 8 * b + 8, N2 * n : N2 * n + N2] for b in range(2) for n in range(N1)], axis=0
    )


def forward(columns, first, second, twist):
    mid = product(first, split(columns))
    real, imag = [], []
    for k in range(N1):
        zr = mid[8 * k : 8 * k + 8]
        zi = mid[256 + 8 * k : 256 + 8 * k + 8]
        c, s = twist[0, k : k + 1, :], twist[1, k : k + 1, :]
        real.append(zr * c + zi * s)
        imag.append(zi * c - zr * s)
    turned = jnp.concatenate([jnp.concatenate(real, 0), jnp.concatenate(imag, 0)], axis=1)
    return product(second, split(turned), ACROSS)


def backward(modes, last, second_back, untwist):
    mid = product(second_back, split(modes))
    zr, zi = mid[:N2], mid[N2:]
    c, s = untwist[0], untwist[1]
    turned = jnp.concatenate([zr * c - zi * s, zr * s + zi * c], axis=1)
    return product(last, split(turned), ACROSS)


def pair(ref):
    return ref[0], ref[1]


def diff_x(plane):
    return pltpu.roll(plane, NX - 1, 1) - pltpu.roll(plane, 1, 1)


def diff_y(plane):
    return pltpu.roll(plane, NY - 1, 0) - pltpu.roll(plane, 1, 0)


def send_kernel(wind, damping, state, past, first, second, twist, out):
    first, second = pair(first), pair(second)
    for which, source in enumerate((state, past)):
        for index in range(3):
            if index == 0:
                plane = diff_x(source[0, 0]) + diff_y(source[1, 0])
            else:
                plane = source[index + 1, 0]
            modes = forward(tiles(plane), first, second, twist)
            for part in range(4):
                block = modes[N2 * (part // 2) : N2 * (part // 2) + N2, 128 * (part % 2) : 128 * (part % 2) + 128]
                out[pl.ds(12 * which + 4 * index + part, N2, stride=ROWS_IN), :] = block
    lane = lax.broadcasted_iota(jnp.int32, (N2, 128), 1)
    out[pl.ds(24, N2, stride=ROWS_IN), :] = jnp.where(lane < 64, damping[0], wind[0])


def weight(section, table, step):
    row = section[step]
    value = jnp.where(row == 3, table[3], 0.0)
    for entry in range(3):
        value = jnp.where(row == entry, table[entry], value)
    return value


def local_kernel(wind, damping, section, state, past, first, last, second, second_back, twist, untwist, out):
    total_now = weight(section, NOW, 0)
    total_past = weight(section, PAST, 0)
    for step in range(1, SUBSTEPS):
        total_now = total_now + weight(section, NOW, step)
        total_past = total_past + weight(section, PAST, step)
    k = lax.broadcasted_iota(jnp.int32, (N2, 256), 0) * N1 + lax.broadcasted_iota(jnp.int32, (N2, 256), 1) // KAP
    fold = jnp.minimum(k, NX - k).astype(f32) * (2.0 / NX)
    fold = fold * fold
    signed = jnp.where(k > NX // 2, k - NX, k)
    signed = jnp.where(k == NX // 2, 0, signed).astype(f32) * (2.0 * math.pi / NX)
    damp = (fold * fold) * (damping[0] * -1.0)
    drift = signed * wind[0]
    for index in range(2):
        modes = forward(tiles(state[index, 0]), pair(first), pair(second), twist)
        fr, fi = modes[:N2], modes[N2:]
        scaled = jnp.concatenate([damp * fr + drift * fi, damp * fi - drift * fr], axis=0)
        slow = backward(scaled, pair(last), pair(second_back), untwist)
        for b in range(2):
            for n in range(N1):
                rows, cols = slice(8 * b, 8 * b + 8), slice(N2 * n, N2 * n + N2)
                piece = slow[8 * (b * N1 + n) : 8 * (b * N1 + n) + 8]
                out[index, rows, cols] = state[index, 0, rows, cols] + FAST * (
                    total_now * piece + total_past * past[index, 0, rows, cols]
                )


def column_kernel(section, lanes, inverse, got, out, chi, slow, up, press, total):
    zero = jnp.zeros((8, 128), f32)
    params = got[pl.ds(24, NZ, stride=ROWS_IN), :]
    damping, wind = params[:, 0:1], params[:, 64:65]

    def plane(which, index, part):
        return got[pl.ds(12 * which + 4 * index + part, NZ, stride=ROWS_IN), :]

    for tile in range(2):
        at = slice(128 * tile, 128 * tile + 128)
        damp = -damping * lanes[0:1, at]
        drift = wind * lanes[1:2, at]
        for index in range(3):
            fr, fi = plane(0, index, tile), plane(0, index, 2 + tile)
            slow[index, tile] = damp * fr + drift * fi
            slow[index, 2 + tile] = damp * fi - drift * fr
            if index == 0:
                chi[tile] = fr
                chi[2 + tile] = fi
    inv = split(inverse[...])
    for part in range(4):
        upright = jnp.concatenate([plane(0, 1, part), plane(0, 2, part)], axis=0)
        solved = product(inv, split(upright))
        up[part, 8 : 8 + NZ] = solved[:NZ]
        press[part, 8 : 8 + NZ] = solved[NZ:]
        total[part] = jnp.zeros((NZ, 128), f32)
        for ref in (up, press):
            ref[part, 0:8] = zero
            ref[part, 8 + NZ : 16 + NZ] = zero

    def step_body(step, carry):
        now = weight(section, NOW, step) * FAST
        then = weight(section, PAST, step) * FAST
        for part in range(4):
            at = slice(128 * (part % 2), 128 * (part % 2) + 128)
            coupling = lanes[2:3, at]
            p = press[part, 8 : 8 + NZ]
            fresh = chi[part] + coupling * p + (now * slow[0, part] + then * plane(1, 0, part))
            chi[part] = fresh
            total[part] = total[part] + p
            up[part, 8 : 8 + NZ] = (
                up[part, 8 : 8 + NZ]
                - HALF * (press[part, 9 : 9 + NZ] - press[part, 7 : 7 + NZ])
                + (now * slow[1, part] + then * plane(1, 1, part))
            )
            press[part, 8 : 8 + NZ] = (
                p
                - HALF * (fresh + (up[part, 9 : 9 + NZ] - up[part, 7 : 7 + NZ]))
                + (now * slow[2, part] + then * plane(1, 2, part))
            )
        return carry

    lax.fori_loop(0, SUBSTEPS, step_body, 0)
    for part in range(4):
        out[pl.ds(part, NZ, stride=ROWS_OUT), :] = total[part]
        out[pl.ds(4 + part, NZ, stride=ROWS_OUT), :] = up[part, 8 : 8 + NZ]
        out[pl.ds(8 + part, NZ, stride=ROWS_OUT), :] = press[part, 8 : 8 + NZ]


def finish_kernel(got, side, last, second_back, untwist, out):
    for index in range(3):
        parts = [got[pl.ds(4 * index + part, N2, stride=ROWS_OUT), :] for part in range(4)]
        modes = jnp.concatenate(
            [jnp.concatenate(parts[:2], axis=1), jnp.concatenate(parts[2:], axis=1)], axis=0
        )
        real = backward(modes, pair(last), pair(second_back), untwist)
        if index:
            for b in range(2):
                for n in range(N1):
                    out[index + 1, 0, 8 * b : 8 * b + 8, N2 * n : N2 * n + N2] = real[
                        8 * (b * N1 + n) : 8 * (b * N1 + n) + 8
                    ]
        else:
            plane = jnp.concatenate(
                [
                    jnp.concatenate([real[8 * (b * N1 + n) : 8 * (b * N1 + n) + 8] for n in range(N1)], axis=1)
                    for b in range(2)
                ],
                axis=0,
            )
            out[0, 0] = side[0] - HALF * diff_x(plane)
            out[1, 0] = side[1] - HALF * diff_y(plane)


def lane_tables(index):
    k = index * N1 + jnp.arange(256, dtype=jnp.int32) // KAP
    wavenum = jnp.minimum(k, NX - k).astype(f32) * (2.0 / NX)
    wavenum = wavenum * wavenum
    signed = jnp.where(k > NX // 2, k - NX, k)
    signed = jnp.where(k == NX // 2, 0, signed).astype(f32) * (2.0 * math.pi / NX)
    sx = jnp.sin(k.astype(f32) * (2.0 * math.pi / NX))
    sy = jnp.sin((jnp.arange(256) % KAP).astype(f32) * (2.0 * math.pi / NY))
    coupling = (4.0 * HALF) * (sx * sx + sy * sy)
    rows = [wavenum * wavenum, signed, coupling]
    return jnp.stack(rows + [jnp.zeros_like(coupling)] * 5)


VMEM = pl.BlockSpec(memory_space=pltpu.VMEM)
SMEM = pl.BlockSpec(memory_space=pltpu.SMEM)


def local(state, past_slow, mean_wind, damping, vertical_inverse, section):
    axes = ("px", "py")
    message = pl.pallas_call(
        send_kernel,
        out_shape=jax.ShapeDtypeStruct((NZ * ROWS_IN, 128), f32),
        in_specs=[SMEM, SMEM] + [VMEM] * 5,
        out_specs=VMEM,
        name="send",
    )(mean_wind, damping, state, past_slow, FIRST, SECOND, TWIST)
    got = lax.all_to_all(message.reshape(NZ, ROWS_IN, 1, 128), axes, split_axis=0, concat_axis=0, tiled=True)
    side = pl.pallas_call(
        local_kernel,
        out_shape=jax.ShapeDtypeStruct((2, NY, NX), f32),
        in_specs=[SMEM, SMEM, SMEM] + [VMEM] * 8,
        out_specs=VMEM,
        cost_estimate=pl.CostEstimate(flops=8_000_000_000, bytes_accessed=4_000_000, transcendentals=0),
        name="side",
    )(mean_wind, damping, section, state, past_slow, FIRST, LAST, SECOND, SECOND_BACK, TWIST, UNTWIST)
    lanes = lane_tables(lax.axis_index(axes))
    padded = pltpu.VMEM((4, NZ + 16, 128), f32)
    solved = pl.pallas_call(
        column_kernel,
        out_shape=jax.ShapeDtypeStruct((NZ * ROWS_OUT, 128), f32),
        in_specs=[SMEM] + [VMEM] * 3,
        out_specs=VMEM,
        scratch_shapes=[
            pltpu.VMEM((4, NZ, 128), f32),
            pltpu.VMEM((3, 4, NZ, 128), f32),
            padded,
            padded,
            pltpu.VMEM((4, NZ, 128), f32),
        ],
        name="columns",
    )(section, lanes, vertical_inverse, got.reshape(NZ * ROWS_IN, 128))
    back = lax.all_to_all(
        solved.reshape(NZ, 3, 4, 128), axes, split_axis=0, concat_axis=0, tiled=True
    )
    return pl.pallas_call(
        finish_kernel,
        out_shape=jax.ShapeDtypeStruct((4, 1, NY, NX), f32),
        in_specs=[VMEM] * 5,
        out_specs=VMEM,
        name="finish",
    )(back.reshape(NZ * ROWS_OUT, 128), side, LAST, SECOND_BACK, UNTWIST)


def solution(mesh):
    in_specs = (
        P(None, ("px", "py"), None, None),
        P(None, ("px", "py"), None, None),
        P(("px", "py")),
        P(("px", "py")),
        P(),
        P(),
    )
    out_specs = P(None, ("px", "py"), None, None)
    return jax.shard_map(local, mesh=mesh, in_specs=in_specs, out_specs=out_specs, check_vma=False)
```

profile of v0, /device:TPU:1, one launch (start us, length us, event | category | flops | bytes accessed | tf_op | source)
XLA Modules:
  0.0 82.2 jit_solution(1713422785295586756)
XLA Ops:
  1.3 10.2 %send.1 = f32[3200,128]{1,0:T(8,128)} custom-call(f32[1]{0:T(128)S(6)} %copy.14.wind, f32[1]{0:T(128)S(6)} %copy.15.damping, f32[4,1,16,4096]{3,2,1,0:T(8,128)} %state.3, f32[4,1,16,4096]{3,2,1,0:T(8,128)} %past.3, bf16[2,512,512]{2,1,0:T(8,128)(2,1)} %constant.76.clone.first, bf16[2,256,256]{2,1,0:T(8,128)(2,1)} %constant.77.clone.second, ...), custom_call_target="tpu_custom_call" | custom-call | tf_op jit(solution)/shard_map/send/pallas_call | solution.py:268
  11.5 11.5 %all-to-all-start = ((f32[128,25,1,128]{3,2,1,0:T(1,128)}), f32[128,25,1,128]{3,2,1,0:T(1,128)S(1)}, u32[]{:S(2)}, u32[]{:S(2)}) async-start(f32[128,25,1,128]{3,2,1,0:T(1,128)} %bitcast.5), calls=%async_computation | async-start | bytes 3276800 | tf_op jit(solution)/shard_map/all_to_all | solution.py:275
  23.0 0.1 fusion.5
  23.1 0.6 stack.10.lanes
  23.7 24.8 %all-to-all-done = f32[128,25,1,128]{3,2,1,0:T(1,128)S(1)} async-done(((f32[128,25,1,128]{3,2,1,0:T(1,128)}), f32[128,25,1,128]{3,2,1,0:T(1,128)S(1)}, u32[]{:S(2)}, u32[]{:S(2)}) %all-to-all-start) | async-done | bytes 1638432 | tf_op jit(solution)/shard_map/all_to_all | solution.py:275
  48.5 0.0 copy-start
  48.5 1.2 %copy-done = f32[128,25,1,128]{3,2,1,0:T(1,128)} copy-done((f32[128,25,1,128]{3,2,1,0:T(1,128)}, f32[128,25,1,128]{3,2,1,0:T(1,128)S(1)}, u32[]{:S(2)}) %copy-start) | copy-done | bytes 1638424
  49.7 5.3 %columns.1 = f32[1536,128]{1,0:T(8,128)} custom-call(s32[8]{0:T(128)} %section.3, f32[8,256]{1,0:T(8,128)} %stack.10.lanes, f32[256,256]{1,0:T(8,128)} %inverse.1, f32[3200,128]{1,0:T(8,128)} %bitcast.4), custom_call_target="tpu_custom_call" | custom-call | tf_op jit(solution)/shard_map/columns/pallas_call | solution.py:286
  55.0 4.6 %all-to-all-start.1 = ((f32[128,3,4,128]{3,2,1,0:T(4,128)}), f32[128,3,4,128]{3,2,1,0:T(4,128)S(1)}, u32[]{:S(2)}, u32[]{:S(2)}) async-start(f32[128,3,4,128]{3,2,1,0:T(4,128)} %bitcast.6), calls=%async_computation.1 | async-start | bytes 1572864 | tf_op jit(solution)/shard_map/all_to_all | solution.py:300
  59.6 6.9 %side.1 = f32[2,16,4096]{2,1,0:T(8,128)} custom-call(f32[1]{0:T(128)S(6)} %copy.14.wind, f32[1]{0:T(128)S(6)} %copy.15.damping, s32[8]{0:T(128)} %section.3, f32[4,1,16,4096]{3,2,1,0:T(8,128)} %state.3, f32[4,1,16,4096]{3,2,1,0:T(8,128)} %past.3, bf16[2,512,512]{2,1,0:T(8,128)(2,1)} %constant.76.clone.first, bf16[2,512,512]{2,1,0:T(8,128)(2,1)} %constant.79.clone.last, ...), custom_call_target="tpu_custom_call" | custom-call | flops 8000000000 | bytes 4000000 | tf_op jit(solution)/shard_map/side/pallas_call | solution.py:276
  66.5 9.9 %all-to-all-done.1 = f32[128,3,4,128]{3,2,1,0:T(4,128)S(1)} async-done(((f32[128,3,4,128]{3,2,1,0:T(4,128)}), f32[128,3,4,128]{3,2,1,0:T(4,128)S(1)}, u32[]{:S(2)}, u32[]{:S(2)}) %all-to-all-start.1) | async-done | bytes 786464 | tf_op jit(solution)/shard_map/all_to_all | solution.py:300
  76.4 0.0 copy-start.1
  76.4 0.9 %copy-done.1 = f32[128,3,4,128]{3,2,1,0:T(4,128)} copy-done((f32[128,3,4,128]{3,2,1,0:T(4,128)}, f32[128,3,4,128]{3,2,1,0:T(4,128)S(1)}, u32[]{:S(2)}) %copy-start.1) | copy-done | bytes 786456
  77.3 4.9 %finish.1 = f32[4,1,16,4096]{3,2,1,0:T(8,128)} custom-call(f32[1536,128]{1,0:T(8,128)} %bitcast.7, f32[2,16,4096]{2,1,0:T(8,128)} %side.1, bf16[2,512,512]{2,1,0:T(8,128)(2,1)} %constant.79.clone.last, bf16[2,256,256]{2,1,0:T(8,128)(2,1)} %constant.80.clone.second_back, f32[2,128,256]{2,1,0:T(8,128)} %constant.81.clone.untwist), custom_call_target="tpu_custom_call" | custom-call | tf_op jit(solution)/shard_map/finish/pallas_call | solution.py:303
  (3 shorter events, 0.0 us)
Async XLA Ops:
  11.5 37.0 %all-to-all-start = ((f32[128,25,1,128]{3,2,1,0:T(1,128)}), f32[128,25,1,128]{3,2,1,0:T(1,128)S(1)}, u32[]{:S(2)}, u32[]{:S(2)}) async-start(f32[128,25,1,128]{3,2,1,0:T(1,128)} %bitcast.5), calls=%async_computation | async-start | bytes 3276800 | tf_op jit(solution)/shard_map/all_to_all | solution.py:275
  48.5 1.2 %copy-start = (f32[128,25,1,128]{3,2,1,0:T(1,128)}, f32[128,25,1,128]{3,2,1,0:T(1,128)S(1)}, u32[]{:S(2)}) copy-start(f32[128,25,1,128]{3,2,1,0:T(1,128)S(1)} %all-to-all-done) | copy-start | bytes 4915204
  55.0 21.5 %all-to-all-start.1 = ((f32[128,3,4,128]{3,2,1,0:T(4,128)}), f32[128,3,4,128]{3,2,1,0:T(4,128)S(1)}, u32[]{:S(2)}, u32[]{:S(2)}) async-start(f32[128,3,4,128]{3,2,1,0:T(4,128)} %bitcast.6), calls=%async_computation.1 | async-start | bytes 1572864 | tf_op jit(solution)/shard_map/all_to_all | solution.py:300
  76.4 0.9 %copy-start.1 = (f32[128,3,4,128]{3,2,1,0:T(4,128)}, f32[128,3,4,128]{3,2,1,0:T(4,128)S(1)}, u32[]{:S(2)}) copy-start(f32[128,3,4,128]{3,2,1,0:T(4,128)S(1)} %all-to-all-done.1) | copy-start | bytes 2359300
where the time goes:
time: 82.6 us; the launch traced here: 82.2 us
  waiting for transfers between devices  34.7 us (42%)
  Pallas kernels  27.3 us (33%)
  starting transfers between devices  16.1 us (19%)
  local copies, waits for them, and re-layouts  2.68 us (3%)
  between operations  1.35 us (2%)
    all_to_all x1, waiting for transfers between devices, local(): lax.all_to_all(message.reshape(NZ, ROWS_IN, 1, 128), axes, split_axis=0,...  24.8 us
    all_to_all x1, starting transfers between devices, local(): lax.all_to_all(message.reshape(NZ, ROWS_IN, 1, 128), axes, split_axis=0,...  11.5 us
    pallas_call x1, Pallas kernels, local(): pl.pallas_call(send_kernel, out_shape=jax.ShapeDtypeStruct((NZ * ROWS_IN,...  10.2 us
    all_to_all x1, waiting for transfers between devices, local(): lax.all_to_all(solved.reshape(NZ, 3, 4, 128), axes, split_axis=0, concat_...  9.93 us
    pallas_call x1, Pallas kernels, local(): pl.pallas_call(local_kernel, out_shape=jax.ShapeDtypeStruct((2, NY, NX),...  6.89 us
    pallas_call x1, Pallas kernels, local(): pl.pallas_call(column_kernel, out_shape=jax.ShapeDtypeStruct((NZ * ROWS_O...  5.3 us
    pallas_call x1, Pallas kernels, local(): pl.pallas_call(finish_kernel, out_shape=jax.ShapeDtypeStruct((4, 1, NY, N...  4.89 us
    all_to_all x1, starting transfers between devices, local(): lax.all_to_all(solved.reshape(NZ, 3, 4, 128), axes, split_axis=0, concat_...  4.63 us
  transfers between devices with their start and end apart: 2, of which 2 were waited for; matrix products, arithmetic and copies ran while one was open for 1% of the time, Pallas kernels for 8%

commit v1 on v0

v1 whole, which is shorter than its diff:
```python
import math

import jax
import jax.numpy as jnp
import numpy as np
from jax import lax
from jax.experimental import pallas as pl
from jax.experimental.pallas import tpu as pltpu
from jax.sharding import PartitionSpec as P

SUBSTEPS = 8
NX, NY, NZ = 4096, 16, 128
N1, N2 = 32, 128
HN = N1 // 2
KAP = NY // 2
HALF = 0.275
FAST = 1.0 / SUBSTEPS
NOW = (-1.0, 2.0, 0.5, 1.5)
PAST = (1.0, -0.5, 0.25, -1.0)
CHUNKS = ((0, 1),)

f32 = jnp.float32
bf16 = jnp.bfloat16


def thrice(table):
    high = np.asarray(jnp.asarray(table, f32).astype(bf16))
    low = np.asarray(jnp.asarray(np.asarray(table, np.float64) - high.astype(np.float64), bf16))
    return np.concatenate([high, low, high], axis=-1)


def tables():
    y = np.arange(NY)
    kap = np.arange(KAP)
    qa = np.cos(2 * np.pi * kap[:, None] * y[None, :] / NY) * math.sqrt(2.0 / NY)
    qb = np.sin(2 * np.pi * kap[:, None] * y[None, :] / NY) * math.sqrt(2.0 / NY)
    qa[0] = 1.0 / math.sqrt(NY)
    qb[0] = (-1.0) ** y / math.sqrt(NY)
    q = qa + 1j * qb
    n1 = np.arange(HN)
    n2 = np.arange(N2)
    firsts, lasts, twists, untwists = [], [], [], []
    for parity in range(2):
        k1 = 2 * np.arange(HN) + parity
        dft1 = np.exp(-2j * np.pi * (k1[:, None] * n1[None, :] % N1) / N1)
        stage = np.einsum("kn,cy->kcny", dft1, q).reshape(HN, KAP, HN, 2, 8)
        stage = stage.transpose(0, 1, 3, 2, 4).reshape(HN * KAP, 2 * HN * 8)
        first = np.concatenate([stage.real, stage.imag], 0)
        firsts.append(thrice(first))
        lasts.append(thrice(first.T / NX))
        turn = 2 * np.pi * (k1[:, None] * n2[None, :]) / NX
        twists.append(np.stack([np.cos(turn), np.sin(turn)]))
        wide = np.repeat(turn.T, KAP, axis=1)
        untwists.append(np.stack([np.cos(wide), np.sin(wide)]))
    angle = 2 * np.pi * (n2[:, None] * n2[None, :] % N2) / N2
    cos, sin = np.cos(angle), np.sin(angle)
    second = np.block([[cos, sin], [-sin, cos]])
    return (
        np.stack(firsts),
        np.stack(lasts),
        thrice(second),
        thrice(second.T),
        np.stack(twists).astype(np.float32),
        np.stack(untwists).astype(np.float32),
    )


FIRST, LAST, SECOND, SECOND_BACK, TWIST, UNTWIST = tables()


def stacked(value, axis):
    high = value.astype(bf16)
    low = (value - high.astype(f32)).astype(bf16)
    return jnp.concatenate([high, high, low], axis=axis)


def product(left, right):
    return lax.dot_general(left, stacked(right, 0), (((1,), (0,)), ((), ())), preferred_element_type=f32)


def product_across(left, right):
    return lax.dot_general(left, stacked(right, 1), (((1,), (1,)), ((), ())), preferred_element_type=f32)


def butterfly(plane, parity):
    parts = []
    for b in range(2):
        rows = slice(8 * b, 8 * b + 8)
        for n in range(HN):
            near = plane[rows, N2 * n : N2 * n + N2]
            far = plane[rows, N2 * (n + HN) : N2 * (n + HN) + N2]
            parts.append(near - far if parity else near + far)
    return jnp.concatenate(parts, axis=0)


def forward(planes, parity, first, second, twist):
    columns = jnp.concatenate([butterfly(plane, parity) for plane in planes], axis=1)
    mid = product(first[parity], columns)
    turned = []
    for index in range(2):
        at = slice(N2 * index, N2 * index + N2)
        real, imag = [], []
        for m in range(HN):
            zr, zi = mid[8 * m : 8 * m + 8, at], mid[128 + 8 * m : 128 + 8 * m + 8, at]
            c, s = twist[parity, 0, m : m + 1, :], twist[parity, 1, m : m + 1, :]
            real.append(zr * c + zi * s)
            imag.append(zi * c - zr * s)
        turned.append(jnp.concatenate([jnp.concatenate(real, 0), jnp.concatenate(imag, 0)], axis=1))
    return product_across(second[...], jnp.concatenate(turned, axis=0))


def backward(modes, last, second_back, untwist):
    sides = []
    for parity in range(2):
        mid = product(second_back[...], modes[parity])
        turned = []
        for index in range(mid.shape[1] // 128):
            at = slice(128 * index, 128 * index + 128)
            zr, zi = mid[:N2, at], mid[N2:, at]
            c, s = untwist[parity, 0], untwist[parity, 1]
            turned.append(jnp.concatenate([zr * c - zi * s, zr * s + zi * c], axis=1))
        sides.append(product_across(last[parity], jnp.concatenate(turned, axis=0)))
    return sides


def real_tiles(sides, index):
    at = slice(128 * index, 128 * index + 128)
    for b in range(2):
        for n in range(HN):
            here = slice(8 * (b * HN + n), 8 * (b * HN + n) + 8)
            even, odd = sides[0][here, at], sides[1][here, at]
            rows = slice(8 * b, 8 * b + 8)
            yield rows, slice(N2 * n, N2 * n + N2), even + odd
            yield rows, slice(N2 * (n + HN), N2 * (n + HN) + N2), even - odd


def diff_x(plane):
    return pltpu.roll(plane, NX - 1, 1) - pltpu.roll(plane, 1, 1)


def diff_y(plane):
    return pltpu.roll(plane, NY - 1, 0) - pltpu.roll(plane, 1, 0)


def rows_in(parities):
    return 12 * len(parities) + (1 if 0 in parities else 0)


def rows_out(parities):
    return 6 * len(parities)


def row_in(parities, which, index, parity, part):
    return 12 * parities.index(parity) + 6 * which + 2 * index + part


def row_out(parities, index, parity, part):
    return 6 * parities.index(parity) + 2 * index + part


def send_kernel(parities, wind, damping, state, past, first, second, twist, out, here, then, one, two, tw, sems):
    copies = {}
    order = [("one", first, one), ("s2", state.at[2, 0], here.at[2]), ("s3", state.at[3, 0], here.at[3])]
    order += [("tw", twist, tw), ("two", second, two)]
    order += [("p2", past.at[2, 0], then.at[2]), ("p3", past.at[3, 0], then.at[3])]
    order += [("s0", state.at[0, 0], here.at[0]), ("s1", state.at[1, 0], here.at[1])]
    order += [("p0", past.at[0, 0], then.at[0]), ("p1", past.at[1, 0], then.at[1])]
    for number, (name, source, target) in enumerate(order):
        copies[name] = pltpu.make_async_copy(source, target, sems.at[number])
        copies[name].start()
    stride = rows_in(parities)

    def emit(pair, planes):
        for parity in parities:
            modes = forward(planes, parity, one, two, tw)
            for slot, (which, index) in enumerate(pair):
                for part in range(2):
                    block = modes[N2 * part : N2 * part + N2, 128 * slot : 128 * slot + 128]
                    out[pl.ds(row_in(parities, which, index, parity, part), N2, stride=stride), :] = block

    if 0 in parities:
        lane = lax.broadcasted_iota(jnp.int32, (N2, 128), 1)
        out[pl.ds(stride - 1, N2, stride=stride), :] = jnp.where(lane < 64, damping[0], wind[0])
    for name in ("one", "s2", "s3", "tw", "two"):
        copies[name].wait()
    emit(((0, 1), (0, 2)), (here[2], here[3]))
    for name in ("p2", "p3"):
        copies[name].wait()
    emit(((1, 1), (1, 2)), (then[2], then[3]))
    for name in ("s0", "s1", "p0", "p1"):
        copies[name].wait()
    emit(((0, 0), (1, 0)), (diff_x(here[0]) + diff_y(here[1]), diff_x(then[0]) + diff_y(then[1])))


def weight(section, table, step):
    row = section[step]
    value = jnp.where(row == 3, table[3], 0.0)
    for entry in range(3):
        value = jnp.where(row == entry, table[entry], value)
    return value


def local_kernel(wind, damping, section, state, past, first, last, second, second_back, twist, untwist, out):
    total_now = weight(section, NOW, 0)
    total_past = weight(section, PAST, 0)
    for step in range(1, SUBSTEPS):
        total_now = total_now + weight(section, NOW, step)
        total_past = total_past + weight(section, PAST, step)
    scaled = []
    for parity in range(2):
        lane = lax.broadcasted_iota(jnp.int32, (N2, 256), 1) % 128
        k = lax.broadcasted_iota(jnp.int32, (N2, 256), 0) * N1 + 2 * (lane // KAP) + parity
        fold = jnp.minimum(k, NX - k).astype(f32) * (2.0 / NX)
        fold = fold * fold
        signed = jnp.where(k > NX // 2, k - NX, k)
        signed = jnp.where(k == NX // 2, 0, signed).astype(f32) * (2.0 * math.pi / NX)
        damp = (fold * fold) * (damping[0] * -1.0)
        drift = signed * wind[0]
        modes = forward((state[0, 0], state[1, 0]), parity, first, second, twist)
        fr, fi = modes[:N2], modes[N2:]
        scaled.append(jnp.concatenate([damp * fr + drift * fi, damp * fi - drift * fr], axis=0))
    sides = backward(scaled, last, second_back, untwist)
    for index in range(2):
        for rows, cols, slow in real_tiles(sides, index):
            out[index, rows, cols] = state[index, 0, rows, cols] + FAST * (
                total_now * slow + total_past * past[index, 0, rows, cols]
            )


def lane_tables(index, parity):
    lane = lax.broadcasted_iota(jnp.int32, (8, 128), 1)
    k = index * N1 + 2 * (lane // KAP) + parity
    fold = jnp.minimum(k, NX - k).astype(f32) * (2.0 / NX)
    fold = fold * fold
    signed = jnp.where(k > NX // 2, k - NX, k)
    signed = jnp.where(k == NX // 2, 0, signed).astype(f32) * (2.0 * math.pi / NX)
    sx = jnp.sin(k.astype(f32) * (2.0 * math.pi / NX))
    sy = jnp.sin((lane % KAP).astype(f32) * (2.0 * math.pi / NY))
    coupling = (4.0 * HALF) * (sx * sx + sy * sy)
    return (fold * fold)[0:1], signed[0:1], coupling[0:1]


def column_kernel(parities, section, index, inverse, *refs):
    params, (got, out, chi, slow, up, press, total, inv_here, sem) = refs[0], refs[-9:]
    fetch = pltpu.make_async_copy(inverse, inv_here, sem)
    fetch.start()
    lanes = {parity: lane_tables(index[0], parity) for parity in parities}
    zero = jnp.zeros((8, 128), f32)
    stride, stride_out = rows_in(parities), rows_out(parities)
    first_stride = rows_in(CHUNKS[0])
    level = params[pl.ds(first_stride - 1, NZ, stride=first_stride), :]
    damping, wind = level[:, 0:1], level[:, 64:65]
    slots = [(parity, part) for parity in parities for part in range(2)]

    def plane(which, index, slot):
        return got[pl.ds(row_in(parities, which, index, *slot), NZ, stride=stride), :]

    for place in range(0, len(slots), 2):
        parity = slots[place][0]
        damp = -damping * lanes[parity][0]
        drift = wind * lanes[parity][1]
        for index in range(3):
            fr, fi = plane(0, index, slots[place]), plane(0, index, slots[place + 1])
            slow[index, place] = damp * fr + drift * fi
            slow[index, place + 1] = damp * fi - drift * fr
            if index == 0:
                chi[place] = fr
                chi[place + 1] = fi
    fetch.wait()
    high = inv_here[...].astype(bf16)
    low = (inv_here[...] - high.astype(f32)).astype(bf16)
    inv = jnp.concatenate([high, low, high], axis=1)
    upright = jnp.concatenate(
        [jnp.concatenate([plane(0, index, slot) for slot in slots], axis=1) for index in (1, 2)], axis=0
    )
    solved = product(inv, upright)
    for place in range(len(slots)):
        up[place, 8 : 8 + NZ] = solved[:NZ, 128 * place : 128 * place + 128]
        press[place, 8 : 8 + NZ] = solved[NZ:, 128 * place : 128 * place + 128]
        total[place] = jnp.zeros((NZ, 128), f32)
        for ref in (up, press):
            ref[place, 0:8] = zero
            ref[place, 8 + NZ : 16 + NZ] = zero

    def step_body(step, carry):
        now = weight(section, NOW, step) * FAST
        then = weight(section, PAST, step) * FAST
        for place, slot in enumerate(slots):
            coupling = lanes[slot[0]][2]
            p = press[place, 8 : 8 + NZ]
            fresh = chi[place] + coupling * p + (now * slow[0, place] + then * plane(1, 0, slot))
            chi[place] = fresh
            total[place] = total[place] + p
            up[place, 8 : 8 + NZ] = (
                up[place, 8 : 8 + NZ]
                - HALF * (press[place, 9 : 9 + NZ] - press[place, 7 : 7 + NZ])
                + (now * slow[1, place] + then * plane(1, 1, slot))
            )
            press[place, 8 : 8 + NZ] = (
                p
                - HALF * (fresh + (up[place, 9 : 9 + NZ] - up[place, 7 : 7 + NZ]))
                + (now * slow[2, place] + then * plane(1, 2, slot))
            )
        return carry

    lax.fori_loop(0, SUBSTEPS, step_body, 0)
    for place, slot in enumerate(slots):
        out[pl.ds(row_out(parities, 0, *slot), NZ, stride=stride_out), :] = total[place]
        out[pl.ds(row_out(parities, 1, *slot), NZ, stride=stride_out), :] = up[place, 8 : 8 + NZ]
        out[pl.ds(row_out(parities, 2, *slot), NZ, stride=stride_out), :] = press[place, 8 : 8 + NZ]


def finish_kernel(*refs):
    got = refs[: len(CHUNKS)]
    side, last, second_back, untwist, out, done, plane, sems = refs[len(CHUNKS) :]

    def modes_of(indices):
        modes = []
        for parity in range(2):
            (chunk,) = [c for c, parities in enumerate(CHUNKS) if parity in parities]
            parities = CHUNKS[chunk]
            cols = [
                jnp.concatenate(
                    [
                        got[chunk][pl.ds(row_out(parities, index, parity, part), N2, stride=rows_out(parities)), :]
                        for part in range(2)
                    ],
                    axis=0,
                )
                for index in indices
            ]
            modes.append(jnp.concatenate(cols, axis=1) if len(cols) > 1 else cols[0])
        return modes

    copies = [pltpu.make_async_copy(done.at[c], out.at[c, 0], sems.at[c]) for c in range(4)]
    sides = backward(modes_of((1, 2)), last, second_back, untwist)
    for index in range(2):
        for rows, cols, value in real_tiles(sides, index):
            done[2 + index, rows, cols] = value
        copies[2 + index].start()
    for rows, cols, value in real_tiles(backward(modes_of((0,)), last, second_back, untwist), 0):
        plane[rows, cols] = value
    done[1] = side[1] - HALF * diff_y(plane[...])
    copies[1].start()
    done[0] = side[0] - HALF * diff_x(plane[...])
    copies[0].start()
    for copy in copies:
        copy.wait()


VMEM = pl.BlockSpec(memory_space=pltpu.VMEM)
SMEM = pl.BlockSpec(memory_space=pltpu.SMEM)
ANY = pl.BlockSpec(memory_space=pl.ANY)


def near(array):
    return pltpu.with_memory_space_constraint(array, pltpu.VMEM)


def local(state, past_slow, mean_wind, damping, vertical_inverse, section):
    axes = ("px", "py")
    arrived = []
    for parities in CHUNKS:
        rows = rows_in(parities)
        message = pl.pallas_call(
            lambda *refs, parities=parities: send_kernel(parities, *refs),
            out_shape=pltpu.VMEM((NZ * rows, 128), f32),
            in_specs=[SMEM, SMEM] + [ANY] * 5,
            out_specs=VMEM,
            scratch_shapes=[
                pltpu.VMEM((4, NY, NX), f32),
                pltpu.VMEM((4, NY, NX), f32),
                pltpu.VMEM(FIRST.shape, bf16),
                pltpu.VMEM(SECOND.shape, bf16),
                pltpu.VMEM(TWIST.shape, f32),
                pltpu.SemaphoreType.DMA((11,)),
            ],
            name="send",
        )(mean_wind, damping, state, past_slow, FIRST, SECOND, TWIST)
        moved = lax.all_to_all(message.reshape(NZ, rows, 1, 128), axes, split_axis=0, concat_axis=0, tiled=True)
        arrived.append(near(moved.reshape(NZ * rows, 128)))
    side = pl.pallas_call(
        local_kernel,
        out_shape=pltpu.VMEM((2, NY, NX), f32),
        in_specs=[SMEM, SMEM, SMEM] + [VMEM] * 8,
        out_specs=VMEM,
        cost_estimate=pl.CostEstimate(flops=8_000_000_000, bytes_accessed=4_000_000, transcendentals=0),
        name="side",
    )(mean_wind, damping, section, state, past_slow, FIRST, LAST, SECOND, SECOND_BACK, TWIST, UNTWIST)
    place = lax.axis_index(axes).astype(jnp.int32).reshape(1)
    returned = []
    for chunk, parities in enumerate(CHUNKS):
        slots, rows = 2 * len(parities), rows_out(parities)
        padded = pltpu.VMEM((slots, NZ + 16, 128), f32)
        solved = pl.pallas_call(
            lambda *refs, parities=parities: column_kernel(parities, *refs),
            out_shape=pltpu.VMEM((NZ * rows, 128), f32),
            in_specs=[SMEM, SMEM, ANY] + [VMEM] * (1 + chunk),
            out_specs=VMEM,
            scratch_shapes=[
                pltpu.VMEM((slots, NZ, 128), f32),
                pltpu.VMEM((3, slots, NZ, 128), f32),
                padded,
                padded,
                pltpu.VMEM((slots, NZ, 128), f32),
                pltpu.VMEM((2 * NZ, 2 * NZ), f32),
                pltpu.SemaphoreType.DMA,
            ],
            name="columns",
        )(section, place, vertical_inverse, *arrived[: chunk + 1])
        back = lax.all_to_all(
            solved.reshape(NZ, rows // 2, 2, 128), axes, split_axis=0, concat_axis=0, tiled=True
        )
        returned.append(near(back.reshape(NZ * rows, 128)))
    return pl.pallas_call(
        finish_kernel,
        out_shape=jax.ShapeDtypeStruct((4, 1, NY, NX), f32),
        in_specs=[VMEM] * (len(CHUNKS) + 4),
        out_specs=ANY,
        scratch_shapes=[
            pltpu.VMEM((4, NY, NX), f32),
            pltpu.VMEM((NY, NX), f32),
            pltpu.SemaphoreType.DMA((4,)),
        ],
        name="finish",
    )(*returned, near(side), near(LAST), near(SECOND_BACK), near(UNTWIST))


def solution(mesh):
    in_specs = (
        P(None, ("px", "py"), None, None),
        P(None, ("px", "py"), None, None),
        P(("px", "py")),
        P(("px", "py")),
        P(),
        P(),
    )
    out_specs = P(None, ("px", "py"), None, None)
    return jax.shard_map(local, mesh=mesh, in_specs=in_specs, out_specs=out_specs, check_vma=False)
```

time: 82.6 us -> 73.8 us (0.89)
  Pallas kernels: 27.3 us -> 17.7 us
  waiting for transfers between devices: 34.7 us -> 38.2 us
  local copies, waits for them, and re-layouts: 2.68 us -> 0.02 us
    pallas_call x3, Pallas kernels: 22.4 us -> 15 us  [the longest x1 5.78 us: local(): pl.pallas_call(lambda *refs, parities=parities: send_kernel(parities, *re...]
    all_to_all x2, waiting for transfers between devices: 34.7 us -> 38.2 us  [the longest x1 25.5 us: local(): lax.all_to_all(message.reshape(NZ, rows, 1, 128), axes, split_axis=0, con...]
    pallas_call x1, Pallas kernels: 4.89 us -> 2.7 us  [local(): pl.pallas_call(finish_kernel, out_shape=jax.ShapeDtypeStruct((4, 1, NY, N...]
    unnamed x4 -> x6, local copies, waits for them, and re-layouts: 2.06 us -> 0.02 us
  transfers between devices with their start and end apart: 2 -> 2, of which waited for: 2 -> 2; matrix products, arithmetic and copies ran while one was open for 1% -> 0% of each run, Pallas kernels for 8% -> 6%
where the time goes in v1:
time: 73.8 us; the launch traced here: 73.5 us
  waiting for transfers between devices  38.2 us (52%)
  Pallas kernels  17.7 us (24%)
  starting transfers between devices  16.1 us (22%)
  between operations  1.37 us (2%)
    all_to_all x1, waiting for transfers between devices, local(): lax.all_to_all(message.reshape(NZ, rows, 1, 128), axes, split_axis=0, con...  25.5 us
    all_to_all x1, waiting for transfers between devices, local(): lax.all_to_all(solved.reshape(NZ, rows // 2, 2, 128), axes, split_axis=0,...  12.7 us
    all_to_all x1, starting transfers between devices, local(): lax.all_to_all(message.reshape(NZ, rows, 1, 128), axes, split_axis=0, con...  11.5 us
    pallas_call x1, Pallas kernels, local(): pl.pallas_call(lambda *refs, parities=parities: send_kernel(parities, *re...  5.78 us
    pallas_call x1, Pallas kernels, local(): pl.pallas_call(lambda *refs, parities=parities: column_kernel(parities, *...  5.17 us
    all_to_all x1, starting transfers between devices, local(): lax.all_to_all(solved.reshape(NZ, rows // 2, 2, 128), axes, split_axis=0,...  4.65 us
    pallas_call x1, Pallas kernels, local(): pl.pallas_call(local_kernel, out_shape=pltpu.VMEM((2, NY, NX), f32), in_s...  4.09 us
    pallas_call x1, Pallas kernels, local(): pl.pallas_call(finish_kernel, out_shape=jax.ShapeDtypeStruct((4, 1, NY, N...  2.7 us
  transfers between devices with their start and end apart: 2, of which 2 were waited for; matrix products, arithmetic and copies ran while one was open for 0% of the time, Pallas kernels for 6%

profile of v1, /device:TPU:1, one launch (start us, length us, event | category | flops | bytes accessed | tf_op | source)
XLA Modules:
  0.0 73.5 jit_solution(2353220447345069756)
XLA Ops:
  1.3 5.8 %send.1 = f32[3200,128]{1,0:T(8,128)} custom-call(f32[1]{0:T(128)S(6)} %copy.14.refs_0_.wind, f32[1]{0:T(128)S(6)} %copy.15.refs_1_.damping, f32[4,1,16,4096]{3,2,1,0:T(8,128)} %state.1, f32[4,1,16,4096]{3,2,1,0:T(8,128)} %past.1, bf16[2,256,768]{2,1,0:T(8,128)(2,1)} %constant.23.clone.refs_4_.first, bf16[256,768]{1,0:T(8,128)(2,1)} %constant.24.clone.refs_5_.second, ...), custom_call_target="tpu_custom_call" | custom-call | tf_op jit(solution)/shard_map/send/pallas_call | solution.py:365
  7.1 11.5 %all-to-all-start = ((f32[128,25,1,128]{3,2,1,0:T(1,128)}), f32[128,25,1,128]{3,2,1,0:T(1,128)S(1)}, u32[]{:S(2)}, u32[]{:S(2)}) async-start(f32[128,25,1,128]{3,2,1,0:T(1,128)} %bitcast.1), calls=%async_computation | async-start | bytes 3276800 | tf_op jit(solution)/shard_map/all_to_all | solution.py:380
  18.6 25.5 %all-to-all-done = f32[128,25,1,128]{3,2,1,0:T(1,128)S(1)} async-done(((f32[128,25,1,128]{3,2,1,0:T(1,128)}), f32[128,25,1,128]{3,2,1,0:T(1,128)S(1)}, u32[]{:S(2)}, u32[]{:S(2)}) %all-to-all-start) | async-done | bytes 1638432 | tf_op jit(solution)/shard_map/all_to_all | solution.py:380
  44.1 5.2 %columns.1 = f32[1536,128]{1,0:T(8,128)} custom-call(s32[8]{0:T(128)} %section.1, s32[1]{0:T(128)} %bitcast.refs_1_, f32[256,256]{1,0:T(8,128)} %refs_2_.4, f32[3200,128]{1,0:T(8,128)S(1)} %bitcast.5), custom_call_target="tpu_custom_call" | custom-call | tf_op jit(solution)/shard_map/columns/pallas_call | solution.py:395
  49.3 4.6 %all-to-all-start.1 = ((f32[128,6,2,128]{3,2,1,0:T(2,128)}), f32[128,6,2,128]{3,2,1,0:T(2,128)S(1)}, u32[]{:S(2)}, u32[]{:S(2)}) async-start(f32[128,6,2,128]{3,2,1,0:T(2,128)} %bitcast.3), calls=%async_computation.1 | async-start | bytes 1572864 | tf_op jit(solution)/shard_map/all_to_all | solution.py:411
  53.9 0.0 copy-start
  54.0 0.0 copy-start.1
  54.0 0.0 copy-start.2
  54.0 4.1 %side.1.refs_1_ = f32[2,16,4096]{2,1,0:T(8,128)S(1)} custom-call(f32[1]{0:T(128)S(6)} %copy.14.refs_0_.wind, f32[1]{0:T(128)S(6)} %copy.15.refs_1_.damping, s32[8]{0:T(128)} %section.1, f32[4,1,16,4096]{3,2,1,0:T(8,128)} %state.1, f32[4,1,16,4096]{3,2,1,0:T(8,128)} %past.1, bf16[2,256,768]{2,1,0:T(8,128)(2,1)} %constant.23.clone.refs_4_.first, ...), custom_call_target="tpu_custom_call" | custom-call | flops 8000000000 | bytes 4000000 | tf_op jit(solution)/shard_map/side/pallas_call | solution.py:382
  58.1 12.7 %all-to-all-done.1 = f32[128,6,2,128]{3,2,1,0:T(2,128)S(1)} async-done(((f32[128,6,2,128]{3,2,1,0:T(2,128)}), f32[128,6,2,128]{3,2,1,0:T(2,128)S(1)}, u32[]{:S(2)}, u32[]{:S(2)}) %all-to-all-start.1) | async-done | bytes 786464 | tf_op jit(solution)/shard_map/all_to_all | solution.py:411
  70.8 0.0 copy-done
  70.8 0.0 copy-done.1
  70.8 0.0 copy-done.2
  70.8 2.7 %finish.1 = f32[4,1,16,4096]{3,2,1,0:T(8,128)} custom-call(f32[1536,128]{1,0:T(8,128)S(1)} %bitcast.6, f32[2,16,4096]{2,1,0:T(8,128)S(1)} %side.1.refs_1_, bf16[2,256,768]{2,1,0:T(8,128)(2,1)S(1)} %copy-done, bf16[256,768]{1,0:T(8,128)(2,1)S(1)} %copy-done.1, f32[2,2,128,128]{3,2,1,0:T(8,128)S(1)} %copy-done.2), custom_call_target="tpu_custom_call" | custom-call | tf_op jit(solution)/shard_map/finish/pallas_call | solution.py:415
Async XLA Ops:
  7.1 37.0 %all-to-all-start = ((f32[128,25,1,128]{3,2,1,0:T(1,128)}), f32[128,25,1,128]{3,2,1,0:T(1,128)S(1)}, u32[]{:S(2)}, u32[]{:S(2)}) async-start(f32[128,25,1,128]{3,2,1,0:T(1,128)} %bitcast.1), calls=%async_computation | async-start | bytes 3276800 | tf_op jit(solution)/shard_map/all_to_all | solution.py:380
  49.3 21.5 %all-to-all-start.1 = ((f32[128,6,2,128]{3,2,1,0:T(2,128)}), f32[128,6,2,128]{3,2,1,0:T(2,128)S(1)}, u32[]{:S(2)}, u32[]{:S(2)}) async-start(f32[128,6,2,128]{3,2,1,0:T(2,128)} %bitcast.3), calls=%async_computation.1 | async-start | bytes 1572864 | tf_op jit(solution)/shard_map/all_to_all | solution.py:411
  53.9 16.8 %copy-start = (bf16[2,256,768]{2,1,0:T(8,128)(2,1)S(1)}, bf16[2,256,768]{2,1,0:T(8,128)(2,1)}, u32[]{:S(2)}) copy-start(bf16[2,256,768]{2,1,0:T(8,128)(2,1)} %constant.26.clone.last.refs_2_) | copy-start | bytes 2359300
  54.0 16.8 %copy-start.1 = (bf16[256,768]{1,0:T(8,128)(2,1)S(1)}, bf16[256,768]{1,0:T(8,128)(2,1)}, u32[]{:S(2)}) copy-start(bf16[256,768]{1,0:T(8,128)(2,1)} %constant.27.clone.second_back.refs_3_) | copy-start | bytes 1179652
  54.0 16.8 %copy-start.2 = (f32[2,2,128,128]{3,2,1,0:T(8,128)S(1)}, f32[2,2,128,128]{3,2,1,0:T(8,128)}, u32[]{:S(2)}) copy-start(f32[2,2,128,128]{3,2,1,0:T(8,128)} %constant.28.clone.untwist.refs_4_) | copy-start | bytes 786436

commit v2 on v1

v2 whole, which is shorter than its diff:
```python
import math

import jax
import jax.numpy as jnp
import numpy as np
from jax import lax
from jax.experimental import pallas as pl
from jax.experimental.pallas import tpu as pltpu
from jax.sharding import PartitionSpec as P

SUBSTEPS = 8
NX, NY, NZ = 4096, 16, 128
N1, N2 = 32, 128
HN = N1 // 2
KAP = NY // 2
HALF = 0.275
FAST = 1.0 / SUBSTEPS
NOW = (-1.0, 2.0, 0.5, 1.5)
PAST = (1.0, -0.5, 0.25, -1.0)
BOTH = (0, 1)

f32 = jnp.float32
bf16 = jnp.bfloat16


def thrice(table):
    high = np.asarray(jnp.asarray(table, f32).astype(bf16))
    low = np.asarray(jnp.asarray(np.asarray(table, np.float64) - high.astype(np.float64), bf16))
    return np.concatenate([high, low, high], axis=-1)


def tables():
    y = np.arange(NY)
    kap = np.arange(KAP)
    qa = np.cos(2 * np.pi * kap[:, None] * y[None, :] / NY) * math.sqrt(2.0 / NY)
    qb = np.sin(2 * np.pi * kap[:, None] * y[None, :] / NY) * math.sqrt(2.0 / NY)
    qa[0] = 1.0 / math.sqrt(NY)
    qb[0] = (-1.0) ** y / math.sqrt(NY)
    q = qa + 1j * qb
    n1 = np.arange(HN)
    n2 = np.arange(N2)
    firsts, lasts, twists, untwists = [], [], [], []
    for parity in range(2):
        k1 = 2 * np.arange(HN) + parity
        dft1 = np.exp(-2j * np.pi * (k1[:, None] * n1[None, :] % N1) / N1)
        stage = np.einsum("kn,cy->kcny", dft1, q).reshape(HN, KAP, HN, 2, 8)
        stage = stage.transpose(0, 1, 3, 2, 4).reshape(HN * KAP, 2 * HN * 8)
        first = np.concatenate([stage.real, stage.imag], 0)
        firsts.append(thrice(first))
        lasts.append(thrice(first.T / NX))
        turn = 2 * np.pi * (k1[:, None] * n2[None, :]) / NX
        twists.append(np.stack([np.cos(turn), np.sin(turn)]))
        wide = np.repeat(turn.T, KAP, axis=1)
        untwists.append(np.stack([np.cos(wide), np.sin(wide)]))
    angle = 2 * np.pi * (n2[:, None] * n2[None, :] % N2) / N2
    cos, sin = np.cos(angle), np.sin(angle)
    second = np.block([[cos, sin], [-sin, cos]])
    k2 = np.arange(N2)
    slopes = []
    for parity in range(2):
        k1 = np.repeat(2 * np.arange(HN) + parity, KAP)
        slopes.append(2 * np.sin(2 * np.pi * (k1[None, :] + N1 * k2[:, None]) / NX))
    across = np.tile(2 * np.sin(2 * np.pi * kap / NY), HN)
    return (
        np.stack(firsts),
        np.stack(lasts),
        thrice(second),
        thrice(second.T),
        np.stack(twists).astype(np.float32),
        np.stack(untwists).astype(np.float32),
        np.stack(slopes).astype(np.float32),
        np.tile(across, (8, 1)).astype(np.float32),
    )


FIRST, LAST, SECOND, SECOND_BACK, TWIST, UNTWIST, SLOPE, ACROSS = tables()


def stacked(value, axis):
    high = value.astype(bf16)
    low = (value - high.astype(f32)).astype(bf16)
    return jnp.concatenate([high, high, low], axis=axis)


def product(left, right):
    return lax.dot_general(left, stacked(right, 0), (((1,), (0,)), ((), ())), preferred_element_type=f32)


def product_across(left, right):
    return lax.dot_general(left, stacked(right, 1), (((1,), (1,)), ((), ())), preferred_element_type=f32)


def butterfly(plane, parity):
    parts = []
    for b in range(2):
        rows = slice(8 * b, 8 * b + 8)
        for n in range(HN):
            near = plane[rows, N2 * n : N2 * n + N2]
            far = plane[rows, N2 * (n + HN) : N2 * (n + HN) + N2]
            parts.append(near - far if parity else near + far)
    return jnp.concatenate(parts, axis=0)


def forward(planes, parity, first, second, twist):
    columns = jnp.concatenate([butterfly(plane, parity) for plane in planes], axis=1)
    mid = product(first[parity], columns)
    turned = []
    for index in range(2):
        at = slice(N2 * index, N2 * index + N2)
        real, imag = [], []
        for m in range(HN):
            zr, zi = mid[8 * m : 8 * m + 8, at], mid[128 + 8 * m : 128 + 8 * m + 8, at]
            c, s = twist[parity, 0, m : m + 1, :], twist[parity, 1, m : m + 1, :]
            real.append(zr * c + zi * s)
            imag.append(zi * c - zr * s)
        turned.append(jnp.concatenate([jnp.concatenate(real, 0), jnp.concatenate(imag, 0)], axis=1))
    return product_across(second[...], jnp.concatenate(turned, axis=0))


def backward(modes, last, second_back, untwist):
    sides = []
    for parity in range(2):
        mid = product(second_back[...], modes[parity])
        turned = []
        for index in range(mid.shape[1] // 128):
            at = slice(128 * index, 128 * index + 128)
            zr, zi = mid[:N2, at], mid[N2:, at]
            c, s = untwist[parity, 0], untwist[parity, 1]
            turned.append(jnp.concatenate([zr * c - zi * s, zr * s + zi * c], axis=1))
        sides.append(product_across(last[parity], jnp.concatenate(turned, axis=0)))
    return sides


def real_tiles(sides, index):
    at = slice(128 * index, 128 * index + 128)
    for b in range(2):
        for n in range(HN):
            here = slice(8 * (b * HN + n), 8 * (b * HN + n) + 8)
            even, odd = sides[0][here, at], sides[1][here, at]
            rows = slice(8 * b, 8 * b + 8)
            yield rows, slice(N2 * n, N2 * n + N2), even + odd
            yield rows, slice(N2 * (n + HN), N2 * (n + HN) + N2), even - odd


def rows_in(parities):
    return 12 * len(parities) + (1 if 0 in parities else 0)


def rows_out(parities):
    return 6 * len(parities)


def row_in(parities, which, index, parity, part):
    return 12 * parities.index(parity) + 6 * which + 2 * index + part


def row_out(parities, index, parity, part):
    return 6 * parities.index(parity) + 2 * index + part


def weight(section, table, step):
    row = section[step]
    value = jnp.where(row == 3, table[3], 0.0)
    for entry in range(3):
        value = jnp.where(row == entry, table[entry], value)
    return value


def times_i(slope, value):
    return jnp.concatenate([-slope * value[N2:], slope * value[:N2]], axis=0)


def send_kernel(
    wind, damping, section, state, past, first, second, twist, slope, across, out, kept, here, then, one, two, tw, sl, ac, sems
):
    copies = {}
    order = [("one", first, one), ("s2", state.at[2, 0], here.at[2]), ("s3", state.at[3, 0], here.at[3])]
    order += [("tw", twist, tw), ("two", second, two)]
    order += [("p2", past.at[2, 0], then.at[2]), ("p3", past.at[3, 0], then.at[3])]
    order += [("s0", state.at[0, 0], here.at[0]), ("s1", state.at[1, 0], here.at[1])]
    order += [("sl", slope, sl), ("ac", across, ac)]
    order += [("p0", past.at[0, 0], then.at[0]), ("p1", past.at[1, 0], then.at[1])]
    for number, (name, source, target) in enumerate(order):
        copies[name] = pltpu.make_async_copy(source, target, sems.at[number])
        copies[name].start()
    stride = rows_in(BOTH)

    def put(which, index, parity, modes):
        for part in range(2):
            rows = pl.ds(row_in(BOTH, which, index, parity, part), N2, stride=stride)
            out[rows, :] = modes[N2 * part : N2 * part + N2]

    lane = lax.broadcasted_iota(jnp.int32, (N2, 128), 1)
    out[pl.ds(stride - 1, N2, stride=stride), :] = jnp.where(lane < 64, damping[0], wind[0])
    total_now = weight(section, NOW, 0)
    total_past = weight(section, PAST, 0)
    for step in range(1, SUBSTEPS):
        total_now = total_now + weight(section, NOW, step)
        total_past = total_past + weight(section, PAST, step)
    total_now = total_now * FAST
    total_past = total_past * FAST
    for name in ("one", "s2", "s3", "tw", "two"):
        copies[name].wait()
    for parity in range(2):
        modes = forward((here[2], here[3]), parity, one, two, tw)
        put(0, 1, parity, modes[:, :128])
        put(0, 2, parity, modes[:, 128:])
    for name in ("p2", "p3"):
        copies[name].wait()
    for parity in range(2):
        modes = forward((then[2], then[3]), parity, one, two, tw)
        put(1, 1, parity, modes[:, :128])
        put(1, 2, parity, modes[:, 128:])
    for name in ("s0", "s1", "sl", "ac", "p0", "p1"):
        copies[name].wait()
    for parity in range(2):
        modes = forward((here[0], here[1]), parity, one, two, tw)
        earlier = forward((then[0], then[1]), parity, one, two, tw)
        steep, aside = sl[parity], ac[0:1]
        put(0, 0, parity, times_i(steep, modes[:, :128]) - times_i(aside, modes[:, 128:]))
        put(1, 0, parity, times_i(steep, earlier[:, :128]) - times_i(aside, earlier[:, 128:]))
        k = lax.broadcasted_iota(jnp.int32, (N2, 128), 0) * N1 + 2 * (lane // KAP) + parity
        fold = jnp.minimum(k, NX - k).astype(f32) * (2.0 / NX)
        fold = fold * fold
        signed = jnp.where(k > NX // 2, k - NX, k)
        signed = jnp.where(k == NX // 2, 0, signed).astype(f32) * (2.0 * math.pi / NX)
        keep = 1.0 - (fold * fold) * (damping[0] * total_now)
        drift = signed * (wind[0] * total_now)
        for index in range(2):
            at = slice(128 * index, 128 * index + 128)
            fr, fi = modes[:N2, at], modes[N2:, at]
            kept[parity, :N2, at] = (keep * fr + drift * fi) + total_past * earlier[:N2, at]
            kept[parity, N2:, at] = (keep * fi - drift * fr) + total_past * earlier[N2:, at]


def lane_tables(index, parity):
    lane = lax.broadcasted_iota(jnp.int32, (8, 128), 1)
    k = index * N1 + 2 * (lane // KAP) + parity
    fold = jnp.minimum(k, NX - k).astype(f32) * (2.0 / NX)
    fold = fold * fold
    signed = jnp.where(k > NX // 2, k - NX, k)
    signed = jnp.where(k == NX // 2, 0, signed).astype(f32) * (2.0 * math.pi / NX)
    sx = jnp.sin(k.astype(f32) * (2.0 * math.pi / NX))
    sy = jnp.sin((lane % KAP).astype(f32) * (2.0 * math.pi / NY))
    coupling = (4.0 * HALF) * (sx * sx + sy * sy)
    return (fold * fold)[0:1], signed[0:1], coupling[0:1]


def column_kernel(parities, section, inverse, *refs):
    params, (got, out, chi, slow, up, press, total) = refs[0], refs[-7:]
    lanes = {parity: lane_tables(lax.axis_index(("px", "py")), parity) for parity in parities}
    zero = jnp.zeros((8, 128), f32)
    stride, stride_out = rows_in(parities), rows_out(parities)
    first_stride = rows_in(BOTH)
    level = params[pl.ds(first_stride - 1, NZ, stride=first_stride), :]
    damping, wind = level[:, 0:1], level[:, 64:65]
    slots = [(parity, part) for parity in parities for part in range(2)]

    def plane(which, index, slot):
        return got[pl.ds(row_in(parities, which, index, *slot), NZ, stride=stride), :]

    for place in range(0, len(slots), 2):
        parity = slots[place][0]
        damp = -damping * lanes[parity][0]
        drift = wind * lanes[parity][1]
        for index in range(3):
            fr, fi = plane(0, index, slots[place]), plane(0, index, slots[place + 1])
            slow[index, place] = damp * fr + drift * fi
            slow[index, place + 1] = damp * fi - drift * fr
            if index == 0:
                chi[place] = fr
                chi[place + 1] = fi
    high = inverse[...].astype(bf16)
    low = (inverse[...] - high.astype(f32)).astype(bf16)
    inv = jnp.concatenate([high, low, high], axis=1)
    upright = jnp.concatenate(
        [jnp.concatenate([plane(0, index, slot) for slot in slots], axis=1) for index in (1, 2)], axis=0
    )
    solved = product(inv, upright)
    for place in range(len(slots)):
        up[place, 8 : 8 + NZ] = solved[:NZ, 128 * place : 128 * place + 128]
        press[place, 8 : 8 + NZ] = solved[NZ:, 128 * place : 128 * place + 128]
        total[place] = jnp.zeros((NZ, 128), f32)
        for ref in (up, press):
            ref[place, 0:8] = zero
            ref[place, 8 + NZ : 16 + NZ] = zero

    def step_body(step, carry):
        now = weight(section, NOW, step) * FAST
        then = weight(section, PAST, step) * FAST
        for place, slot in enumerate(slots):
            coupling = lanes[slot[0]][2]
            p = press[place, 8 : 8 + NZ]
            fresh = chi[place] + coupling * p + (now * slow[0, place] + then * plane(1, 0, slot))
            chi[place] = fresh
            total[place] = total[place] + p
            up[place, 8 : 8 + NZ] = (
                up[place, 8 : 8 + NZ]
                - HALF * (press[place, 9 : 9 + NZ] - press[place, 7 : 7 + NZ])
                + (now * slow[1, place] + then * plane(1, 1, slot))
            )
            press[place, 8 : 8 + NZ] = (
                p
                - HALF * (fresh + (up[place, 9 : 9 + NZ] - up[place, 7 : 7 + NZ]))
                + (now * slow[2, place] + then * plane(1, 2, slot))
            )
        return carry

    lax.fori_loop(0, SUBSTEPS, step_body, 0)
    for place, slot in enumerate(slots):
        out[pl.ds(row_out(parities, 0, *slot), NZ, stride=stride_out), :] = total[place]
        out[pl.ds(row_out(parities, 1, *slot), NZ, stride=stride_out), :] = up[place, 8 : 8 + NZ]
        out[pl.ds(row_out(parities, 2, *slot), NZ, stride=stride_out), :] = press[place, 8 : 8 + NZ]


def finish_kernel(got, kept, last, second_back, untwist, slope, across, out, done, sems):
    def modes_of(index, parity):
        rows = [pl.ds(row_out(BOTH, index, parity, part), N2, stride=rows_out(BOTH)) for part in range(2)]
        return jnp.concatenate([got[rows[0], :], got[rows[1], :]], axis=0)

    copies = [pltpu.make_async_copy(done.at[c], out.at[c, 0], sems.at[c]) for c in range(4)]

    def finish(modes, base):
        sides = backward(modes, last, second_back, untwist)
        for index in range(2):
            for rows, cols, value in real_tiles(sides, index):
                done[base + index, rows, cols] = value
            copies[base + index].start()

    finish([jnp.concatenate([modes_of(1, q), modes_of(2, q)], axis=1) for q in BOTH], 2)
    flows = []
    for parity in BOTH:
        total = modes_of(0, parity)
        steep, aside = HALF * slope[parity], HALF * across[0:1]
        flows.append(
            jnp.concatenate(
                [kept[parity, :, :128] - times_i(steep, total), kept[parity, :, 128:] + times_i(aside, total)], axis=1
            )
        )
    finish(flows, 0)
    for copy in copies:
        copy.wait()


VMEM = pl.BlockSpec(memory_space=pltpu.VMEM)
SMEM = pl.BlockSpec(memory_space=pltpu.SMEM)
HBM = pl.BlockSpec(memory_space=pltpu.HBM)
ROOM = pltpu.CompilerParams(vmem_limit_bytes=40 * 2**20)


def near(array):
    return pltpu.with_memory_space_constraint(array, pltpu.VMEM)


def local(state, past_slow, mean_wind, damping, vertical_inverse, section):
    axes = ("px", "py")
    rows = rows_in(BOTH)
    message, kept = pl.pallas_call(
        send_kernel,
        out_shape=[pltpu.VMEM((NZ * rows, 128), f32), pltpu.VMEM((2, 2 * N2, 256), f32)],
        in_specs=[SMEM, SMEM, SMEM] + [HBM] * 7,
        out_specs=[VMEM, VMEM],
        scratch_shapes=[
            pltpu.VMEM((4, NY, NX), f32),
            pltpu.VMEM((4, NY, NX), f32),
            pltpu.VMEM(FIRST.shape, bf16),
            pltpu.VMEM(SECOND.shape, bf16),
            pltpu.VMEM(TWIST.shape, f32),
            pltpu.VMEM(SLOPE.shape, f32),
            pltpu.VMEM(ACROSS.shape, f32),
            pltpu.SemaphoreType.DMA((13,)),
        ],
        name="send",
    )(mean_wind, damping, section, state, past_slow, FIRST, SECOND, TWIST, SLOPE, ACROSS)
    moved = lax.all_to_all(message.reshape(NZ, rows, 1, 128), axes, split_axis=0, concat_axis=0, tiled=True)
    arrived = near(moved.reshape(NZ * rows, 128))
    rows = rows_out(BOTH)
    padded = pltpu.VMEM((4, NZ + 16, 128), f32)
    solved = pl.pallas_call(
        lambda *refs: column_kernel(BOTH, *refs),
        out_shape=pltpu.VMEM((NZ * rows, 128), f32),
        in_specs=[SMEM, VMEM, VMEM],
        out_specs=VMEM,
        scratch_shapes=[
            pltpu.VMEM((4, NZ, 128), f32),
            pltpu.VMEM((3, 4, NZ, 128), f32),
            padded,
            padded,
            pltpu.VMEM((4, NZ, 128), f32),
        ],
        compiler_params=ROOM,
        name="columns",
    )(section, near(vertical_inverse), arrived)
    back = lax.all_to_all(solved.reshape(NZ, rows // 2, 2, 128), axes, split_axis=0, concat_axis=0, tiled=True)
    returned = near(back.reshape(NZ * rows, 128))
    return pl.pallas_call(
        finish_kernel,
        out_shape=jax.ShapeDtypeStruct((4, 1, NY, NX), f32),
        in_specs=[VMEM] * 7,
        out_specs=HBM,
        scratch_shapes=[pltpu.VMEM((4, NY, NX), f32), pltpu.SemaphoreType.DMA((4,))],
        compiler_params=ROOM,
        name="finish",
    )(returned, near(kept), near(LAST), near(SECOND_BACK), near(UNTWIST), near(SLOPE), near(ACROSS))


def solution(mesh):
    in_specs = (
        P(None, ("px", "py"), None, None),
        P(None, ("px", "py"), None, None),
        P(("px", "py")),
        P(("px", "py")),
        P(),
        P(),
    )
    out_specs = P(None, ("px", "py"), None, None)
    return jax.shard_map(local, mesh=mesh, in_specs=in_specs, out_specs=out_specs, check_vma=False)
```

time: 73.8 us -> 70.1 us (0.950)
  blocking collectives: 0 us -> 57.6 us
  waiting for transfers between devices: 38.2 us -> 0 us
  starting transfers between devices: 16.1 us -> 0 us
  Pallas kernels: 17.7 us -> 10.9 us
    all_to_all x0 -> x2, blocking collectives: none -> 57.6 us  [the longest x1 36.8 us: local(): lax.all_to_all(message.reshape(NZ, rows, 1, 128), axes, split_axis=0, con...]
    all_to_all x2 -> x0, waiting for transfers between devices: 38.2 us -> none  [the longest x1 25.5 us: local(): lax.all_to_all(message.reshape(NZ, rows, 1, 128), axes, split_axis=0, con...]
    all_to_all x2 -> x0, starting transfers between devices: 16.1 us -> none  [the longest x1 11.5 us: local(): lax.all_to_all(message.reshape(NZ, rows, 1, 128), axes, split_axis=0, con...]
    pallas_call x3 -> x2, Pallas kernels: 15 us -> 8.68 us  [the longest x1 5.44 us: local(): pl.pallas_call(send_kernel, out_shape=[pltpu.VMEM((NZ * rows, 128), f32),...]
  transfers between devices with their start and end apart: 2 -> 0, of which waited for: 2 -> 0; matrix products, arithmetic and copies ran while one was open for 0% -> 0% of each run, Pallas kernels for 6% -> 0%
where the time goes in v2:
time: 70.1 us; the launch traced here: 70 us
  blocking collectives  57.6 us (82%)
  Pallas kernels  10.9 us (16%)
  between operations  1.38 us (2%)
    all_to_all x1, blocking collectives, local(): lax.all_to_all(message.reshape(NZ, rows, 1, 128), axes, split_axis=0, con...  36.8 us
    all_to_all x1, blocking collectives, local(): lax.all_to_all(solved.reshape(NZ, rows // 2, 2, 128), axes, split_axis=0,...  20.8 us
    pallas_call x1, Pallas kernels, local(): pl.pallas_call(send_kernel, out_shape=[pltpu.VMEM((NZ * rows, 128), f32),...  5.44 us
    pallas_call x1, Pallas kernels, local(): pl.pallas_call(lambda *refs: column_kernel(BOTH, *refs), out_shape=pltpu....  3.24 us
    pallas_call x1, Pallas kernels, local(): pl.pallas_call(finish_kernel, out_shape=jax.ShapeDtypeStruct((4, 1, NY, N...  2.24 us

profile of v2, /device:TPU:1, one launch (start us, length us, event | category | flops | bytes accessed | tf_op | source)
XLA Modules:
  0.0 70.0 jit_solution(5193170580125335080)
XLA Ops:
  1.3 5.4 %send.1 = (f32[3200,128]{1,0:T(8,128)S(1)}, f32[2,256,256]{2,1,0:T(8,128)S(1)}) custom-call(f32[1]{0:T(128)S(6)} %copy.16.wind, f32[1]{0:T(128)S(6)} %copy.17.damping, s32[8]{0:T(128)} %refs_0_.1, f32[4,1,16,4096]{3,2,1,0:T(8,128)} %state.1, f32[4,1,16,4096]{3,2,1,0:T(8,128)} %past.1, bf16[2,256,768]{2,1,0:T(8,128)(2,1)} %constant.16.clone.first, ...), custom_call_target="tpu_custom_call" | custom-call | tf_op jit(solution)/shard_map/send/pallas_call | solution.py:358
  6.7 0.0 copy-start.3
  6.8 0.0 copy-start.6
  6.8 36.8 %all_to_all.10 = f32[128,25,1,128]{3,2,1,0:T(1,128)S(1)} all-to-all(f32[128,25,1,128]{3,2,1,0:T(1,128)S(1)} %bitcast.7), channel_id=1, replica_groups=mesh['px'=16,'py'=8] {'px','py'}, dimensions={0} | all-to-all | bytes 3276800 | tf_op jit(solution)/shard_map/all_to_all | solution.py:375
  43.6 0.0 copy-done.3
  43.6 0.0 copy-done.6
  43.6 0.0 copy-start
  43.6 0.0 copy-start.1
  43.6 0.0 copy-start.2
  43.6 0.0 copy-start.4
  43.6 0.0 copy-start.5
  43.6 3.2 %columns.1 = f32[1536,128]{1,0:T(8,128)S(1)} custom-call(s32[8]{0:T(128)S(1)} %copy-done.6, f32[256,256]{1,0:T(8,128)S(1)} %copy-done.3, f32[3200,128]{1,0:T(8,128)S(1)} %bitcast.4), custom_call_target="tpu_custom_call" | custom-call | tf_op jit(solution)/shard_map/columns/pallas_call | solution.py:379
  46.9 20.8 %all_to_all.11 = f32[128,6,2,128]{3,2,1,0:T(2,128)S(1)} all-to-all(f32[128,6,2,128]{3,2,1,0:T(2,128)S(1)} %bitcast.6), channel_id=1, replica_groups=mesh['px'=16,'py'=8] {'px','py'}, dimensions={0} | all-to-all | bytes 1572864 | tf_op jit(solution)/shard_map/all_to_all | solution.py:394
  67.7 0.0 copy-done
  67.7 0.0 copy-done.1
  67.7 0.0 copy-done.2
  67.7 0.0 copy-done.4
  67.7 0.0 copy-done.5
  67.7 2.2 %finish.1 = f32[4,1,16,4096]{3,2,1,0:T(8,128)} custom-call(f32[1536,128]{1,0:T(8,128)S(1)} %bitcast.5, f32[2,256,256]{2,1,0:T(8,128)S(1)} %get-tuple-element.8.kept, bf16[2,256,768]{2,1,0:T(8,128)(2,1)S(1)} %copy-done, bf16[256,768]{1,0:T(8,128)(2,1)S(1)} %copy-done.2, f32[2,2,128,128]{3,2,1,0:T(8,128)S(1)} %copy-done.4, f32[2,128,128]{2,1,0:T(8,128)S(1)} %copy-done.1, ...), custom_call_target="tpu_custom_call" | custom-call | tf_op jit(solution)/shard_map/finish/pallas_call | solution.py:396
Async XLA Ops:
  6.7 36.8 %copy-start.3 = (f32[256,256]{1,0:T(8,128)S(1)}, f32[256,256]{1,0:T(8,128)}, u32[]{:S(2)}) copy-start(f32[256,256]{1,0:T(8,128)} %refs_1_.1) | copy-start | bytes 786436
  6.8 36.8 %copy-start.6 = (s32[8]{0:T(128)S(1)}, s32[8]{0:T(128)}, u32[]{:S(2)}) copy-start(s32[8]{0:T(128)} %refs_0_.1) | copy-start | bytes 100
  43.6 24.1 %copy-start = (bf16[2,256,768]{2,1,0:T(8,128)(2,1)S(1)}, bf16[2,256,768]{2,1,0:T(8,128)(2,1)}, u32[]{:S(2)}) copy-start(bf16[2,256,768]{2,1,0:T(8,128)(2,1)} %constant.21.clone.last) | copy-start | bytes 2359300
  43.6 24.1 %copy-start.1 = (f32[2,128,128]{2,1,0:T(8,128)S(1)}, f32[2,128,128]{2,1,0:T(8,128)}, u32[]{:S(2)}) copy-start(f32[2,128,128]{2,1,0:T(8,128)} %constant.19.clone.slope) | copy-start | bytes 393220
  43.6 24.1 %copy-start.2 = (bf16[256,768]{1,0:T(8,128)(2,1)S(1)}, bf16[256,768]{1,0:T(8,128)(2,1)}, u32[]{:S(2)}) copy-start(bf16[256,768]{1,0:T(8,128)(2,1)} %constant.22.clone.second_back) | copy-start | bytes 1179652
  43.6 24.1 %copy-start.4 = (f32[2,2,128,128]{3,2,1,0:T(8,128)S(1)}, f32[2,2,128,128]{3,2,1,0:T(8,128)}, u32[]{:S(2)}) copy-start(f32[2,2,128,128]{3,2,1,0:T(8,128)} %constant.23.clone.untwist) | copy-start | bytes 786436
  43.6 24.1 %copy-start.5 = (f32[8,128]{1,0:T(8,128)S(1)}, f32[8,128]{1,0:T(8,128)}, u32[]{:S(2)}) copy-start(f32[8,128]{1,0:T(8,128)} %constant.20.clone.across) | copy-start | bytes 12292

commit v3 on v2

--- a/solution.py
+++ b/solution.py
@@ -23,10 +23,10 @@
 bf16 = jnp.bfloat16
 
 
-def thrice(table):
+def halves(table):
     high = np.asarray(jnp.asarray(table, f32).astype(bf16))
     low = np.asarray(jnp.asarray(np.asarray(table, np.float64) - high.astype(np.float64), bf16))
-    return np.concatenate([high, low, high], axis=-1)
+    return np.concatenate([high, low], axis=-1)
 
 
 def tables():
@@ -46,8 +46,8 @@
         stage = np.einsum("kn,cy->kcny", dft1, q).reshape(HN, KAP, HN, 2, 8)
         stage = stage.transpose(0, 1, 3, 2, 4).reshape(HN * KAP, 2 * HN * 8)
         first = np.concatenate([stage.real, stage.imag], 0)
-        firsts.append(thrice(first))
-        lasts.append(thrice(first.T / NX))
+        firsts.append(halves(first))
+        lasts.append(halves(first.T / NX))
         turn = 2 * np.pi * (k1[:, None] * n2[None, :]) / NX
         twists.append(np.stack([np.cos(turn), np.sin(turn)]))
         wide = np.repeat(turn.T, KAP, axis=1)
@@ -64,8 +64,8 @@
     return (
         np.stack(firsts),
         np.stack(lasts),
-        thrice(second),
-        thrice(second.T),
+        halves(second),
+        halves(second.T),
         np.stack(twists).astype(np.float32),
         np.stack(untwists).astype(np.float32),
         np.stack(slopes).astype(np.float32),
@@ -76,18 +76,20 @@
 FIRST, LAST, SECOND, SECOND_BACK, TWIST, UNTWIST, SLOPE, ACROSS = tables()
 
 
-def stacked(value, axis):
-    high = value.astype(bf16)
-    low = (value - high.astype(f32)).astype(bf16)
-    return jnp.concatenate([high, high, low], axis=axis)
-
-
-def product(left, right):
-    return lax.dot_general(left, stacked(right, 0), (((1,), (0,)), ((), ())), preferred_element_type=f32)
+def product(left, right, dims=((1,), (0,))):
+    high = right.astype(bf16)
+    low = (right - high.astype(f32)).astype(bf16)
+
+    def dot(table, data):
+        return lax.dot_general(table, data, (dims, ((), ())), preferred_element_type=f32)
+
+    count = left.shape[0]
+    both = dot(jnp.concatenate([left[:, :256], left[:, 256:]], axis=0), high)
+    return both[:count] + (both[count:] + dot(left[:, :256], low))
 
 
 def product_across(left, right):
-    return lax.dot_general(left, stacked(right, 1), (((1,), (1,)), ((), ())), preferred_element_type=f32)
+    return product(left, right, ((1,), (1,)))
 
 
 def butterfly(plane, parity):
@@ -171,7 +173,29 @@
 
 
 def send_kernel(
-    wind, damping, section, state, past, first, second, twist, slope, across, out, kept, here, then, one, two, tw, sl, ac, sems
+    wind_in,
+    damping_in,
+    section_in,
+    state,
+    past,
+    first,
+    second,
+    twist,
+    slope,
+    across,
+    out,
+    kept,
+    here,
+    then,
+    one,
+    two,
+    tw,
+    sl,
+    ac,
+    wind,
+    damping,
+    section,
+    sems,
 ):
     copies = {}
     order = [("one", first, one), ("s2", state.at[2, 0], here.at[2]), ("s3", state.at[3, 0], here.at[3])]
@@ -180,6 +204,7 @@
     order += [("s0", state.at[0, 0], here.at[0]), ("s1", state.at[1, 0], here.at[1])]
     order += [("sl", slope, sl), ("ac", across, ac)]
     order += [("p0", past.at[0, 0], then.at[0]), ("p1", past.at[1, 0], then.at[1])]
+    order += [("wind", wind_in, wind), ("damping", damping_in, damping), ("section", section_in, section)]
     for number, (name, source, target) in enumerate(order):
         copies[name] = pltpu.make_async_copy(source, target, sems.at[number])
         copies[name].start()
@@ -190,6 +215,16 @@
             rows = pl.ds(row_in(BOTH, which, index, parity, part), N2, stride=stride)
             out[rows, :] = modes[N2 * part : N2 * part + N2]
 
+    for name in copies:
+        copies[name].wait()
+    for parity in range(2):
+        modes = forward((here[2], here[3]), parity, one, two, tw)
+        put(0, 1, parity, modes[:, :128])
+        put(0, 2, parity, modes[:, 128:])
+    for parity in range(2):
+        modes = forward((then[2], then[3]), parity, one, two, tw)
+        put(1, 1, parity, modes[:, :128])
+        put(1, 2, parity, modes[:, 128:])
     lane = lax.broadcasted_iota(jnp.int32, (N2, 128), 1)
     out[pl.ds(stride - 1, N2, stride=stride), :] = jnp.where(lane < 64, damping[0], wind[0])
     total_now = weight(section, NOW, 0)
@@ -199,20 +234,6 @@
         total_past = total_past + weight(section, PAST, step)
     total_now = total_now * FAST
     total_past = total_past * FAST
-    for name in ("one", "s2", "s3", "tw", "two"):
-        copies[name].wait()
-    for parity in range(2):
-        modes = forward((here[2], here[3]), parity, one, two, tw)
-        put(0, 1, parity, modes[:, :128])
-        put(0, 2, parity, modes[:, 128:])
-    for name in ("p2", "p3"):
-        copies[name].wait()
-    for parity in range(2):
-        modes = forward((then[2], then[3]), parity, one, two, tw)
-        put(1, 1, parity, modes[:, :128])
-        put(1, 2, parity, modes[:, 128:])
-    for name in ("s0", "s1", "sl", "ac", "p0", "p1"):
-        copies[name].wait()
     for parity in range(2):
         modes = forward((here[0], here[1]), parity, one, two, tw)
         earlier = forward((then[0], then[1]), parity, one, two, tw)
@@ -246,13 +267,14 @@
     return (fold * fold)[0:1], signed[0:1], coupling[0:1]
 
 
-def column_kernel(parities, section, inverse, *refs):
-    params, (got, out, chi, slow, up, press, total) = refs[0], refs[-7:]
+def column_kernel(parities, section_in, inverse, got, out, chi, slow, up, press, total, section, sem):
+    fetch = pltpu.make_async_copy(section_in, section, sem)
+    fetch.start()
     lanes = {parity: lane_tables(lax.axis_index(("px", "py")), parity) for parity in parities}
     zero = jnp.zeros((8, 128), f32)
     stride, stride_out = rows_in(parities), rows_out(parities)
     first_stride = rows_in(BOTH)
-    level = params[pl.ds(first_stride - 1, NZ, stride=first_stride), :]
+    level = got[pl.ds(first_stride - 1, NZ, stride=first_stride), :]
     damping, wind = level[:, 0:1], level[:, 64:65]
     slots = [(parity, part) for parity in parities for part in range(2)]
 
@@ -272,7 +294,7 @@
                 chi[place + 1] = fi
     high = inverse[...].astype(bf16)
     low = (inverse[...] - high.astype(f32)).astype(bf16)
-    inv = jnp.concatenate([high, low, high], axis=1)
+    inv = jnp.concatenate([high, low], axis=1)
     upright = jnp.concatenate(
         [jnp.concatenate([plane(0, index, slot) for slot in slots], axis=1) for index in (1, 2)], axis=0
     )
@@ -284,6 +306,8 @@
         for ref in (up, press):
             ref[place, 0:8] = zero
             ref[place, 8 + NZ : 16 + NZ] = zero
+
+    fetch.wait()
 
     def step_body(step, carry):
         now = weight(section, NOW, step) * FAST
@@ -343,7 +367,6 @@
 
 
 VMEM = pl.BlockSpec(memory_space=pltpu.VMEM)
-SMEM = pl.BlockSpec(memory_space=pltpu.SMEM)
 HBM = pl.BlockSpec(memory_space=pltpu.HBM)
 ROOM = pltpu.CompilerParams(vmem_limit_bytes=40 * 2**20)
 
@@ -358,7 +381,7 @@
     message, kept = pl.pallas_call(
         send_kernel,
         out_shape=[pltpu.VMEM((NZ * rows, 128), f32), pltpu.VMEM((2, 2 * N2, 256), f32)],
-        in_specs=[SMEM, SMEM, SMEM] + [HBM] * 7,
+        in_specs=[HBM] * 10,
         out_specs=[VMEM, VMEM],
         scratch_shapes=[
             pltpu.VMEM((4, NY, NX), f32),
@@ -368,7 +391,10 @@
             pltpu.VMEM(TWIST.shape, f32),
             pltpu.VMEM(SLOPE.shape, f32),
             pltpu.VMEM(ACROSS.shape, f32),
-            pltpu.SemaphoreType.DMA((13,)),
+            pltpu.SMEM((1,), f32),
+            pltpu.SMEM((1,), f32),
+            pltpu.SMEM((SUBSTEPS,), jnp.int32),
+            pltpu.SemaphoreType.DMA((16,)),
         ],
         name="send",
     )(mean_wind, damping, section, state, past_slow, FIRST, SECOND, TWIST, SLOPE, ACROSS)
@@ -379,7 +405,7 @@
     solved = pl.pallas_call(
         lambda *refs: column_kernel(BOTH, *refs),
         out_shape=pltpu.VMEM((NZ * rows, 128), f32),
-        in_specs=[SMEM, VMEM, VMEM],
+        in_specs=[HBM, VMEM, VMEM],
         out_specs=VMEM,
         scratch_shapes=[
             pltpu.VMEM((4, NZ, 128), f32),
@@ -387,6 +413,8 @@
             padded,
             padded,
             pltpu.VMEM((4, NZ, 128), f32),
+            pltpu.SMEM((SUBSTEPS,), jnp.int32),
+            pltpu.SemaphoreType.DMA,
         ],
         compiler_params=ROOM,
         name="columns",

time: 70.1 us -> 68.4 us (0.976)
  Pallas kernels: 10.9 us -> 9.19 us
    pallas_call x1, Pallas kernels: 5.44 us -> 4.15 us  [local(): pl.pallas_call(send_kernel, out_shape=[pltpu.VMEM((NZ * rows, 128), f32),...]
where the time goes in v3:
time: 68.4 us; the launch traced here: 68.2 us
  blocking collectives  57.6 us (84%)
  Pallas kernels  9.19 us (13%)
  between operations  1.38 us (2%)
    all_to_all x1, blocking collectives, local(): lax.all_to_all(message.reshape(NZ, rows, 1, 128), axes, split_axis=0, con...  36.8 us
    all_to_all x1, blocking collectives, local(): lax.all_to_all(solved.reshape(NZ, rows // 2, 2, 128), axes, split_axis=0,...  20.8 us
    pallas_call x1, Pallas kernels, local(): pl.pallas_call(send_kernel, out_shape=[pltpu.VMEM((NZ * rows, 128), f32),...  4.15 us
    pallas_call x1, Pallas kernels, local(): pl.pallas_call(lambda *refs: column_kernel(BOTH, *refs), out_shape=pltpu....  2.84 us
    pallas_call x1, Pallas kernels, local(): pl.pallas_call(finish_kernel, out_shape=jax.ShapeDtypeStruct((4, 1, NY, N...  2.21 us

profile of v3, /device:TPU:1, one launch (start us, length us, event | category | flops | bytes accessed | tf_op | source)
XLA Modules:
  0.0 68.2 jit_solution(3005543367637452406)
XLA Ops:
  1.3 4.1 %send.1 = (f32[3200,128]{1,0:T(8,128)S(1)}, f32[2,256,256]{2,1,0:T(8,128)S(1)}) custom-call(f32[1]{0:T(128)S(6)} %copy.16.wind_in, f32[1]{0:T(128)S(6)} %copy.17.damping_in, s32[8]{0:T(128)} %refs_0_.1, f32[4,1,16,4096]{3,2,1,0:T(8,128)} %state.1, f32[4,1,16,4096]{3,2,1,0:T(8,128)} %past.1, bf16[2,256,512]{2,1,0:T(8,128)(2,1)} %constant.16.clone.first, ...), custom_call_target="tpu_custom_call" | custom-call | tf_op jit(solution)/shard_map/send/pallas_call | solution.py:381
  5.5 0.0 copy-start.2
  5.5 0.0 copy-start.6
  5.5 36.8 %all_to_all.10 = f32[128,25,1,128]{3,2,1,0:T(1,128)S(1)} all-to-all(f32[128,25,1,128]{3,2,1,0:T(1,128)S(1)} %bitcast.7), channel_id=1, replica_groups=mesh['px'=16,'py'=8] {'px','py'}, dimensions={0} | all-to-all | bytes 3276800 | tf_op jit(solution)/shard_map/all_to_all | solution.py:401
  42.3 0.0 copy-done.2
  42.3 0.0 copy-done.6
  42.3 0.0 copy-start
  42.3 0.0 copy-start.1
  42.3 0.0 copy-start.3
  42.3 0.0 copy-start.4
  42.3 0.0 copy-start.5
  42.3 2.8 %columns.1 = f32[1536,128]{1,0:T(8,128)S(1)} custom-call(s32[8]{0:T(128)S(1)} %copy-done.6, f32[256,256]{1,0:T(8,128)S(1)} %copy-done.2, f32[3200,128]{1,0:T(8,128)S(1)} %bitcast.4), custom_call_target="tpu_custom_call" | custom-call | tf_op jit(solution)/shard_map/columns/pallas_call | solution.py:405
  45.2 20.8 %all_to_all.11 = f32[128,6,2,128]{3,2,1,0:T(2,128)S(1)} all-to-all(f32[128,6,2,128]{3,2,1,0:T(2,128)S(1)} %bitcast.6), channel_id=1, replica_groups=mesh['px'=16,'py'=8] {'px','py'}, dimensions={0} | all-to-all | bytes 1572864 | tf_op jit(solution)/shard_map/all_to_all | solution.py:422
  66.0 0.0 copy-done
  66.0 0.0 copy-done.1
  66.0 0.0 copy-done.3
  66.0 0.0 copy-done.4
  66.0 0.0 copy-done.5
  66.0 2.2 %finish.1 = f32[4,1,16,4096]{3,2,1,0:T(8,128)} custom-call(f32[1536,128]{1,0:T(8,128)S(1)} %bitcast.5, f32[2,256,256]{2,1,0:T(8,128)S(1)} %get-tuple-element.8.kept, bf16[2,256,512]{2,1,0:T(8,128)(2,1)S(1)} %copy-done.1, bf16[256,512]{1,0:T(8,128)(2,1)S(1)} %copy-done.4, f32[2,2,128,128]{3,2,1,0:T(8,128)S(1)} %copy-done.3, f32[2,128,128]{2,1,0:T(8,128)S(1)} %copy-done, ...), custom_call_target="tpu_custom_call" | custom-call | tf_op jit(solution)/shard_map/finish/pallas_call | solution.py:424
Async XLA Ops:
  5.5 36.8 %copy-start.2 = (f32[256,256]{1,0:T(8,128)S(1)}, f32[256,256]{1,0:T(8,128)}, u32[]{:S(2)}) copy-start(f32[256,256]{1,0:T(8,128)} %refs_1_.1) | copy-start | bytes 786436
  5.5 36.8 %copy-start.6 = (s32[8]{0:T(128)S(1)}, s32[8]{0:T(128)}, u32[]{:S(2)}) copy-start(s32[8]{0:T(128)} %refs_0_.1) | copy-start | bytes 100
  42.3 23.7 %copy-start = (f32[2,128,128]{2,1,0:T(8,128)S(1)}, f32[2,128,128]{2,1,0:T(8,128)}, u32[]{:S(2)}) copy-start(f32[2,128,128]{2,1,0:T(8,128)} %constant.19.clone.slope) | copy-start | bytes 393220
  42.3 23.7 %copy-start.1 = (bf16[2,256,512]{2,1,0:T(8,128)(2,1)S(1)}, bf16[2,256,512]{2,1,0:T(8,128)(2,1)}, u32[]{:S(2)}) copy-start(bf16[2,256,512]{2,1,0:T(8,128)(2,1)} %constant.21.clone.last) | copy-start | bytes 1572868
  42.3 23.7 %copy-start.3 = (f32[2,2,128,128]{3,2,1,0:T(8,128)S(1)}, f32[2,2,128,128]{3,2,1,0:T(8,128)}, u32[]{:S(2)}) copy-start(f32[2,2,128,128]{3,2,1,0:T(8,128)} %constant.23.clone.untwist) | copy-start | bytes 786436
  42.3 23.7 %copy-start.4 = (bf16[256,512]{1,0:T(8,128)(2,1)S(1)}, bf16[256,512]{1,0:T(8,128)(2,1)}, u32[]{:S(2)}) copy-start(bf16[256,512]{1,0:T(8,128)(2,1)} %constant.22.clone.second_back) | copy-start | bytes 786436
  42.3 23.7 %copy-start.5 = (f32[8,128]{1,0:T(8,128)S(1)}, f32[8,128]{1,0:T(8,128)}, u32[]{:S(2)}) copy-start(f32[8,128]{1,0:T(8,128)} %constant.20.clone.across) | copy-start | bytes 12292

commit v4 on v3

--- a/solution.py
+++ b/solution.py
@@ -12,6 +12,7 @@
 NX, NY, NZ = 4096, 16, 128
 N1, N2 = 32, 128
 HN = N1 // 2
+TILE = 16
 KAP = NY // 2
 HALF = 0.275
 FAST = 1.0 / SUBSTEPS
@@ -59,8 +60,8 @@
     slopes = []
     for parity in range(2):
         k1 = np.repeat(2 * np.arange(HN) + parity, KAP)
-        slopes.append(2 * np.sin(2 * np.pi * (k1[None, :] + N1 * k2[:, None]) / NX))
-    across = np.tile(2 * np.sin(2 * np.pi * kap / NY), HN)
+        slopes.append(2 * HALF * np.sin(2 * np.pi * (k1[None, :] + N1 * k2[:, None]) / NX))
+    across = np.tile(2 * HALF * np.sin(2 * np.pi * kap / NY), HN)
     return (
         np.stack(firsts),
         np.stack(lasts),
@@ -263,7 +264,7 @@
     signed = jnp.where(k == NX // 2, 0, signed).astype(f32) * (2.0 * math.pi / NX)
     sx = jnp.sin(k.astype(f32) * (2.0 * math.pi / NX))
     sy = jnp.sin((lane % KAP).astype(f32) * (2.0 * math.pi / NY))
-    coupling = (4.0 * HALF) * (sx * sx + sy * sy)
+    coupling = (4.0 * HALF * HALF) * (sx * sx + sy * sy)
     return (fold * fold)[0:1], signed[0:1], coupling[0:1]
 
 
@@ -300,7 +301,7 @@
     )
     solved = product(inv, upright)
     for place in range(len(slots)):
-        up[place, 8 : 8 + NZ] = solved[:NZ, 128 * place : 128 * place + 128]
+        up[place, 8 : 8 + NZ] = HALF * solved[:NZ, 128 * place : 128 * place + 128]
         press[place, 8 : 8 + NZ] = solved[NZ:, 128 * place : 128 * place + 128]
         total[place] = jnp.zeros((NZ, 128), f32)
         for ref in (up, press):
@@ -312,28 +313,39 @@
     def step_body(step, carry):
         now = weight(section, NOW, step) * FAST
         then = weight(section, PAST, step) * FAST
+        now_up, then_up = now * HALF, then * HALF
+
+        def late(which, index, slot, z):
+            return got[pl.ds(row_in(parities, which, index, *slot) + stride * z, TILE, stride=stride), :]
+
         for place, slot in enumerate(slots):
-            coupling = lanes[slot[0]][2]
-            p = press[place, 8 : 8 + NZ]
-            fresh = chi[place] + coupling * p + (now * slow[0, place] + then * plane(1, 0, slot))
-            chi[place] = fresh
-            total[place] = total[place] + p
-            up[place, 8 : 8 + NZ] = (
-                up[place, 8 : 8 + NZ]
-                - HALF * (press[place, 9 : 9 + NZ] - press[place, 7 : 7 + NZ])
-                + (now * slow[1, place] + then * plane(1, 1, slot))
-            )
-            press[place, 8 : 8 + NZ] = (
-                p
-                - HALF * (fresh + (up[place, 9 : 9 + NZ] - up[place, 7 : 7 + NZ]))
-                + (now * slow[2, place] + then * plane(1, 2, slot))
-            )
+            for z in range(0, NZ, TILE):
+                here = slice(z, z + TILE)
+                p = press[place, 8 + z : 8 + z + TILE]
+                total[place, here] = total[place, here] + p
+                chi[place, here] = (
+                    chi[place, here]
+                    + lanes[slot[0]][2] * p
+                    + (now * slow[0, place, here] + then * late(1, 0, slot, z))
+                )
+                up[place, 8 + z : 8 + z + TILE] = (
+                    up[place, 8 + z : 8 + z + TILE]
+                    - (HALF * HALF) * (press[place, 9 + z : 9 + z + TILE] - press[place, 7 + z : 7 + z + TILE])
+                    + (now_up * slow[1, place, here] + then_up * late(1, 1, slot, z))
+                )
+            for z in range(0, NZ, TILE):
+                here = slice(z, z + TILE)
+                press[place, 8 + z : 8 + z + TILE] = (
+                    press[place, 8 + z : 8 + z + TILE]
+                    - (chi[place, here] + (up[place, 9 + z : 9 + z + TILE] - up[place, 7 + z : 7 + z + TILE]))
+                    + (now * slow[2, place, here] + then * late(1, 2, slot, z))
+                )
         return carry
 
     lax.fori_loop(0, SUBSTEPS, step_body, 0)
     for place, slot in enumerate(slots):
         out[pl.ds(row_out(parities, 0, *slot), NZ, stride=stride_out), :] = total[place]
-        out[pl.ds(row_out(parities, 1, *slot), NZ, stride=stride_out), :] = up[place, 8 : 8 + NZ]
+        out[pl.ds(row_out(parities, 1, *slot), NZ, stride=stride_out), :] = up[place, 8 : 8 + NZ] * (1.0 / HALF)
         out[pl.ds(row_out(parities, 2, *slot), NZ, stride=stride_out), :] = press[place, 8 : 8 + NZ]
 
 
@@ -355,7 +367,7 @@
     flows = []
     for parity in BOTH:
         total = modes_of(0, parity)
-        steep, aside = HALF * slope[parity], HALF * across[0:1]
+        steep, aside = slope[parity], across[0:1]
         flows.append(
             jnp.concatenate(
                 [kept[parity, :, :128] - times_i(steep, total), kept[parity, :, 128:] + times_i(aside, total)], axis=1

time: 68.4 us -> 67.9 us (level)
  no operation moved by 1% of the time
where the time goes in v4:
time: 67.9 us; the launch traced here: 67.7 us
  blocking collectives  57.6 us (85%)
  Pallas kernels  8.61 us (13%)
  between operations  1.38 us (2%)
    all_to_all x1, blocking collectives, local(): lax.all_to_all(message.reshape(NZ, rows, 1, 128), axes, split_axis=0, con...  36.8 us
    all_to_all x1, blocking collectives, local(): lax.all_to_all(solved.reshape(NZ, rows // 2, 2, 128), axes, split_axis=0,...  20.8 us
    pallas_call x1, Pallas kernels, local(): pl.pallas_call(send_kernel, out_shape=[pltpu.VMEM((NZ * rows, 128), f32),...  4.15 us
    pallas_call x1, Pallas kernels, local(): pl.pallas_call(lambda *refs: column_kernel(BOTH, *refs), out_shape=pltpu....  2.24 us
    pallas_call x1, Pallas kernels, local(): pl.pallas_call(finish_kernel, out_shape=jax.ShapeDtypeStruct((4, 1, NY, N...  2.22 us

profile of v4, /device:TPU:1, one launch (start us, length us, event | category | flops | bytes accessed | tf_op | source)
XLA Modules:
  0.0 67.7 jit_solution(11349452490398923022)
XLA Ops:
  1.3 4.1 %send.1 = (f32[3200,128]{1,0:T(8,128)S(1)}, f32[2,256,256]{2,1,0:T(8,128)S(1)}) custom-call(f32[1]{0:T(128)S(6)} %copy.16.wind_in, f32[1]{0:T(128)S(6)} %copy.17.damping_in, s32[8]{0:T(128)} %refs_0_.1, f32[4,1,16,4096]{3,2,1,0:T(8,128)} %state.1, f32[4,1,16,4096]{3,2,1,0:T(8,128)} %past.1, bf16[2,256,512]{2,1,0:T(8,128)(2,1)} %constant.16.clone.first, ...), custom_call_target="tpu_custom_call" | custom-call | tf_op jit(solution)/shard_map/send/pallas_call | solution.py:393
  5.5 0.0 copy-start.2
  5.5 0.0 copy-start.6
  5.5 36.8 %all_to_all.10 = f32[128,25,1,128]{3,2,1,0:T(1,128)S(1)} all-to-all(f32[128,25,1,128]{3,2,1,0:T(1,128)S(1)} %bitcast.7), channel_id=1, replica_groups=mesh['px'=16,'py'=8] {'px','py'}, dimensions={0} | all-to-all | bytes 3276800 | tf_op jit(solution)/shard_map/all_to_all | solution.py:413
  42.3 0.0 copy-done.2
  42.3 0.0 copy-done.6
  42.3 0.0 copy-start
  42.3 0.0 copy-start.1
  42.3 0.0 copy-start.3
  42.3 0.0 copy-start.4
  42.3 0.0 copy-start.5
  42.3 2.2 %columns.1 = f32[1536,128]{1,0:T(8,128)S(1)} custom-call(s32[8]{0:T(128)S(1)} %copy-done.6, f32[256,256]{1,0:T(8,128)S(1)} %copy-done.2, f32[3200,128]{1,0:T(8,128)S(1)} %bitcast.4), custom_call_target="tpu_custom_call" | custom-call | tf_op jit(solution)/shard_map/columns/pallas_call | solution.py:417
  44.6 20.8 %all_to_all.11 = f32[128,6,2,128]{3,2,1,0:T(2,128)S(1)} all-to-all(f32[128,6,2,128]{3,2,1,0:T(2,128)S(1)} %bitcast.6), channel_id=1, replica_groups=mesh['px'=16,'py'=8] {'px','py'}, dimensions={0} | all-to-all | bytes 1572864 | tf_op jit(solution)/shard_map/all_to_all | solution.py:434
  65.4 0.0 copy-done
  65.4 0.0 copy-done.1
  65.4 0.0 copy-done.3
  65.4 0.0 copy-done.4
  65.4 0.0 copy-done.5
  65.4 2.2 %finish.1 = f32[4,1,16,4096]{3,2,1,0:T(8,128)} custom-call(f32[1536,128]{1,0:T(8,128)S(1)} %bitcast.5, f32[2,256,256]{2,1,0:T(8,128)S(1)} %get-tuple-element.8.kept, bf16[2,256,512]{2,1,0:T(8,128)(2,1)S(1)} %copy-done.1, bf16[256,512]{1,0:T(8,128)(2,1)S(1)} %copy-done.4, f32[2,2,128,128]{3,2,1,0:T(8,128)S(1)} %copy-done.3, f32[2,128,128]{2,1,0:T(8,128)S(1)} %copy-done, ...), custom_call_target="tpu_custom_call" | custom-call | tf_op jit(solution)/shard_map/finish/pallas_call | solution.py:436
Async XLA Ops:
  5.5 36.8 %copy-start.2 = (f32[256,256]{1,0:T(8,128)S(1)}, f32[256,256]{1,0:T(8,128)}, u32[]{:S(2)}) copy-start(f32[256,256]{1,0:T(8,128)} %refs_1_.1) | copy-start | bytes 786436
  5.5 36.8 %copy-start.6 = (s32[8]{0:T(128)S(1)}, s32[8]{0:T(128)}, u32[]{:S(2)}) copy-start(s32[8]{0:T(128)} %refs_0_.1) | copy-start | bytes 100
  42.3 23.1 %copy-start = (f32[2,128,128]{2,1,0:T(8,128)S(1)}, f32[2,128,128]{2,1,0:T(8,128)}, u32[]{:S(2)}) copy-start(f32[2,128,128]{2,1,0:T(8,128)} %constant.19.clone.slope) | copy-start | bytes 393220
  42.3 23.1 %copy-start.1 = (bf16[2,256,512]{2,1,0:T(8,128)(2,1)S(1)}, bf16[2,256,512]{2,1,0:T(8,128)(2,1)}, u32[]{:S(2)}) copy-start(bf16[2,256,512]{2,1,0:T(8,128)(2,1)} %constant.21.clone.last) | copy-start | bytes 1572868
  42.3 23.1 %copy-start.3 = (f32[2,2,128,128]{3,2,1,0:T(8,128)S(1)}, f32[2,2,128,128]{3,2,1,0:T(8,128)}, u32[]{:S(2)}) copy-start(f32[2,2,128,128]{3,2,1,0:T(8,128)} %constant.23.clone.untwist) | copy-start | bytes 786436
  42.3 23.1 %copy-start.4 = (bf16[256,512]{1,0:T(8,128)(2,1)S(1)}, bf16[256,512]{1,0:T(8,128)(2,1)}, u32[]{:S(2)}) copy-start(bf16[256,512]{1,0:T(8,128)(2,1)} %constant.22.clone.second_back) | copy-start | bytes 786436
  42.3 23.1 %copy-start.5 = (f32[8,128]{1,0:T(8,128)S(1)}, f32[8,128]{1,0:T(8,128)}, u32[]{:S(2)}) copy-start(f32[8,128]{1,0:T(8,128)} %constant.20.clone.across) | copy-start | bytes 12292

commit v5 on v4

--- a/solution.py
+++ b/solution.py
@@ -89,8 +89,16 @@
     return both[:count] + (both[count:] + dot(left[:, :256], low))
 
 
+def deep(left, right, axis, dims):
+    high = right.astype(bf16)
+    low = (right - high.astype(f32)).astype(bf16)
+    table = jnp.concatenate([left[...], left[:, :256]], axis=1)
+    data = jnp.concatenate([high, high, low], axis=axis)
+    return lax.dot_general(table, data, (dims, ((), ())), preferred_element_type=f32)
+
+
 def product_across(left, right):
-    return product(left, right, ((1,), (1,)))
+    return deep(left, right, 1, ((1,), (1,)))
 
 
 def butterfly(plane, parity):
@@ -199,12 +207,8 @@
     sems,
 ):
     copies = {}
-    order = [("one", first, one), ("s2", state.at[2, 0], here.at[2]), ("s3", state.at[3, 0], here.at[3])]
-    order += [("tw", twist, tw), ("two", second, two)]
-    order += [("p2", past.at[2, 0], then.at[2]), ("p3", past.at[3, 0], then.at[3])]
-    order += [("s0", state.at[0, 0], here.at[0]), ("s1", state.at[1, 0], here.at[1])]
-    order += [("sl", slope, sl), ("ac", across, ac)]
-    order += [("p0", past.at[0, 0], then.at[0]), ("p1", past.at[1, 0], then.at[1])]
+    order = [("state", state.at[:, 0], here), ("past", past.at[:, 0], then), ("one", first, one)]
+    order += [("two", second, two), ("slope", slope, sl), ("tw", twist, tw), ("ac", across, ac)]
     order += [("wind", wind_in, wind), ("damping", damping_in, damping), ("section", section_in, section)]
     for number, (name, source, target) in enumerate(order):
         copies[name] = pltpu.make_async_copy(source, target, sems.at[number])
@@ -406,7 +410,7 @@
             pltpu.SMEM((1,), f32),
             pltpu.SMEM((1,), f32),
             pltpu.SMEM((SUBSTEPS,), jnp.int32),
-            pltpu.SemaphoreType.DMA((16,)),
+            pltpu.SemaphoreType.DMA((10,)),
         ],
         name="send",
     )(mean_wind, damping, section, state, past_slow, FIRST, SECOND, TWIST, SLOPE, ACROSS)

time: 67.9 us -> 67.8 us (level)
  no operation moved by 1% of the time
where the time goes in v5:
time: 67.8 us; the launch traced here: 67.6 us
  blocking collectives  57.6 us (85%)
  Pallas kernels  8.54 us (13%)
  between operations  1.38 us (2%)
    all_to_all x1, blocking collectives, local(): lax.all_to_all(message.reshape(NZ, rows, 1, 128), axes, split_axis=0, con...  36.8 us
    all_to_all x1, blocking collectives, local(): lax.all_to_all(solved.reshape(NZ, rows // 2, 2, 128), axes, split_axis=0,...  20.8 us
    pallas_call x1, Pallas kernels, local(): pl.pallas_call(send_kernel, out_shape=[pltpu.VMEM((NZ * rows, 128), f32),...  4.07 us
    pallas_call x1, Pallas kernels, local(): pl.pallas_call(lambda *refs: column_kernel(BOTH, *refs), out_shape=pltpu....  2.24 us
    pallas_call x1, Pallas kernels, local(): pl.pallas_call(finish_kernel, out_shape=jax.ShapeDtypeStruct((4, 1, NY, N...  2.23 us

profile of v5, /device:TPU:1, one launch (start us, length us, event | category | flops | bytes accessed | tf_op | source)
XLA Modules:
  0.0 67.6 jit_solution(3567287643984886645)
XLA Ops:
  1.3 4.1 %send.1 = (f32[3200,128]{1,0:T(8,128)S(1)}, f32[2,256,256]{2,1,0:T(8,128)S(1)}) custom-call(f32[1]{0:T(128)S(6)} %copy.16.wind_in, f32[1]{0:T(128)S(6)} %copy.17.damping_in, s32[8]{0:T(128)} %refs_0_.1, f32[4,1,16,4096]{3,2,1,0:T(8,128)} %state.1, f32[4,1,16,4096]{3,2,1,0:T(8,128)} %past.1, bf16[2,256,512]{2,1,0:T(8,128)(2,1)} %constant.16.clone.first, ...), custom_call_target="tpu_custom_call" | custom-call | tf_op jit(solution)/shard_map/send/pallas_call | solution.py:397
  5.4 0.0 copy-start.2
  5.4 0.0 copy-start.6
  5.4 36.8 %all_to_all.10 = f32[128,25,1,128]{3,2,1,0:T(1,128)S(1)} all-to-all(f32[128,25,1,128]{3,2,1,0:T(1,128)S(1)} %bitcast.7), channel_id=1, replica_groups=mesh['px'=16,'py'=8] {'px','py'}, dimensions={0} | all-to-all | bytes 3276800 | tf_op jit(solution)/shard_map/all_to_all | solution.py:417
  42.2 0.0 copy-done.2
  42.2 0.0 copy-done.6
  42.2 0.0 copy-start
  42.2 0.0 copy-start.1
  42.2 0.0 copy-start.3
  42.2 0.0 copy-start.4
  42.3 0.0 copy-start.5
  42.3 2.2 %columns.1 = f32[1536,128]{1,0:T(8,128)S(1)} custom-call(s32[8]{0:T(128)S(1)} %copy-done.6, f32[256,256]{1,0:T(8,128)S(1)} %copy-done.2, f32[3200,128]{1,0:T(8,128)S(1)} %bitcast.4), custom_call_target="tpu_custom_call" | custom-call | tf_op jit(solution)/shard_map/columns/pallas_call | solution.py:421
  44.5 20.8 %all_to_all.11 = f32[128,6,2,128]{3,2,1,0:T(2,128)S(1)} all-to-all(f32[128,6,2,128]{3,2,1,0:T(2,128)S(1)} %bitcast.6), channel_id=1, replica_groups=mesh['px'=16,'py'=8] {'px','py'}, dimensions={0} | all-to-all | bytes 1572864 | tf_op jit(solution)/shard_map/all_to_all | solution.py:438
  65.3 0.0 copy-done
  65.3 0.0 copy-done.1
  65.3 0.0 copy-done.3
  65.3 0.0 copy-done.4
  65.3 0.0 copy-done.5
  65.4 2.2 %finish.1 = f32[4,1,16,4096]{3,2,1,0:T(8,128)} custom-call(f32[1536,128]{1,0:T(8,128)S(1)} %bitcast.5, f32[2,256,256]{2,1,0:T(8,128)S(1)} %get-tuple-element.8.kept, bf16[2,256,512]{2,1,0:T(8,128)(2,1)S(1)} %copy-done.1, bf16[256,512]{1,0:T(8,128)(2,1)S(1)} %copy-done.4, f32[2,2,128,128]{3,2,1,0:T(8,128)S(1)} %copy-done.3, f32[2,128,128]{2,1,0:T(8,128)S(1)} %copy-done, ...), custom_call_target="tpu_custom_call" | custom-call | tf_op jit(solution)/shard_map/finish/pallas_call | solution.py:440
Async XLA Ops:
  5.4 36.8 %copy-start.2 = (f32[256,256]{1,0:T(8,128)S(1)}, f32[256,256]{1,0:T(8,128)}, u32[]{:S(2)}) copy-start(f32[256,256]{1,0:T(8,128)} %refs_1_.1) | copy-start | bytes 786436
  5.4 36.8 %copy-start.6 = (s32[8]{0:T(128)S(1)}, s32[8]{0:T(128)}, u32[]{:S(2)}) copy-start(s32[8]{0:T(128)} %refs_0_.1) | copy-start | bytes 100
  42.2 23.1 %copy-start = (f32[2,128,128]{2,1,0:T(8,128)S(1)}, f32[2,128,128]{2,1,0:T(8,128)}, u32[]{:S(2)}) copy-start(f32[2,128,128]{2,1,0:T(8,128)} %constant.19.clone.slope) | copy-start | bytes 393220
  42.2 23.1 %copy-start.1 = (bf16[2,256,512]{2,1,0:T(8,128)(2,1)S(1)}, bf16[2,256,512]{2,1,0:T(8,128)(2,1)}, u32[]{:S(2)}) copy-start(bf16[2,256,512]{2,1,0:T(8,128)(2,1)} %constant.21.clone.last) | copy-start | bytes 1572868
  42.2 23.1 %copy-start.3 = (f32[2,2,128,128]{3,2,1,0:T(8,128)S(1)}, f32[2,2,128,128]{3,2,1,0:T(8,128)}, u32[]{:S(2)}) copy-start(f32[2,2,128,128]{3,2,1,0:T(8,128)} %constant.23.clone.untwist) | copy-start | bytes 786436
  42.2 23.1 %copy-start.4 = (bf16[256,512]{1,0:T(8,128)(2,1)S(1)}, bf16[256,512]{1,0:T(8,128)(2,1)}, u32[]{:S(2)}) copy-start(bf16[256,512]{1,0:T(8,128)(2,1)} %constant.22.clone.second_back) | copy-start | bytes 786436
  42.3 23.1 %copy-start.5 = (f32[8,128]{1,0:T(8,128)S(1)}, f32[8,128]{1,0:T(8,128)}, u32[]{:S(2)}) copy-start(f32[8,128]{1,0:T(8,128)} %constant.20.clone.across) | copy-start | bytes 12292
